TPU v7x, 128 devices: a whole 4x4x4 slice. The times are simulated.
128 devices in a mesh: dp: 16 (over y, z_lo, core), ep: 8 (over z_hi, x).
Axes of the slice: x: 4, y: 4, z: 4 (z_hi: 2, z_lo: 2; z = z_hi * 2 + z_lo), core: 2. Of those that a mesh axis runs over, the one named last changes fastest.
Arguments:
- tokens: bfloat16 [16384, 6144], P(('dp', 'ep')), may hold values from -6 to 6
- out_grad: bfloat16 [16384, 6144], P(('dp', 'ep')), may hold values from -0.75 to 0.75
- expert_ids: int32 [16384, 2], P(('dp', 'ep')), may hold values from 0 to 7, all different within a row; in each aligned block of 128 rows (0 to 127, 128 to 255, ...) at most 40 rows name the same one
- route_weight: float32 [16384, 2], P(('dp', 'ep')), may hold values from 0.2 to 1
- w_gate: bfloat16 [8, 6144, 256], P('ep', 'dp'), may hold values from -0.078125 to 0.078125
- w_up: bfloat16 [8, 6144, 256], P('ep', 'dp'), may hold values from -0.078125 to 0.078125
- w_down: bfloat16 [8, 256, 6144], P('ep', None, 'dp'), may hold values from -0.375 to 0.375
Outputs:
- d_tokens: bfloat16 [16384, 6144], P(('dp', 'ep'))
- grad_gate: float32 [8, 6144, 256], P('ep', 'dp')
- grad_up: float32 [8, 6144, 256], P('ep', 'dp')
- grad_down: float32 [8, 256, 6144], P('ep', None, 'dp')
Inputs may be any that keep to these rules, and one draw needn't show every extreme that they name: `expert_ids`: each token names two different experts. Among the 128 tokens of one device (aligned blocks of 128 rows) no expert is named more than 40 times, and in some blocks one expert is named exactly 40 times.
All inputs are finite; a program needn't handle non-finite values.
Results may differ from a plain program's by a relative error of at most 0.0065.
Values may be sent and summed in bfloat16 or wider, within the bound.
A program may use at most 128 MiB of HBM per device.

v0:
```python
import functools

import jax
import jax.numpy as jnp
from jax import lax
from jax.experimental import pallas as pl
from jax.experimental.pallas import tpu as pltpu
from jax.sharding import PartitionSpec as P

MESH = pl.DeviceIdType.MESH
F32, BF16 = jnp.float32, jnp.bfloat16
PEERS = [(dy, dz) for dy in (2, 1, 3, 0) for dz in (1, 0) if (dy, dz) != (0, 0)]


class Spot:
    def __init__(self):
        dp, ep = lax.axis_index("dp"), lax.axis_index("ep")
        self.y, self.zl, self.c = dp // 4, (dp // 2) % 2, dp % 2
        self.zh, self.x = ep // 4, ep % 4
        self.q = dp // 2

    def to(self, y=0, zl=0, c=0, zh=0, x=0):
        dp = (self.y + y) % 4 * 4 + (self.zl + zl) % 2 * 2 + (self.c + c) % 2
        return (dp, (self.zh + zh) % 2 * 4 + (self.x + x) % 4)

    def block(self, y, zl):
        return (self.y + y) % 4 * 2 + (self.zl + zl) % 2

    def expert(self, x, zh):
        return (self.zh + zh) % 2 * 4 + (self.x + x) % 4


class Links:
    def __init__(self, send_sem, recv_sem):
        self.send_sem, self.recv_sem, self.count, self.sent = send_sem, recv_sem, 0, []

    def send(self, src, dst, device):
        n = self.count
        self.count += 1
        copy = pltpu.make_async_remote_copy(
            src_ref=src,
            dst_ref=dst,
            send_sem=self.send_sem.at[n],
            recv_sem=self.recv_sem.at[n],
            device_id=device,
            device_id_type=MESH,
        )
        copy.start()
        self.sent.append(copy)
        return copy

    def finish(self):
        for copy in self.sent:
            copy.wait_send()


def greet(devices):
    barrier = pltpu.get_barrier_semaphore()
    for device in devices:
        pl.semaphore_signal(barrier, inc=1, device_id=device, device_id_type=MESH)
    pl.semaphore_wait(barrier, len(devices))


def add_rows(dst, sources, rows, step=32):
    @pl.loop(0, rows // step)
    def _(i):
        at = pl.ds(pl.multiple_of(i * step, step), step)
        total = sources[0][at, :].astype(F32)
        for source in sources[1:]:
            total = total + source[at, :].astype(F32)
        dst[at, :] = total.astype(dst.dtype)


SPREAD_COPIES = 21 + 1 + 2 + 1 + 3 + 6 + 6 + 4


def spread_kernel(tok, og, ids, w_in, x_out, og_out, ids_out, w_out, send_sem, recv_sem, own_sem):
    me = Spot()
    right, left, core, far = me.to(x=1), me.to(x=3), me.to(c=1), me.to(zh=1)
    greet([me.to(y=dy, zl=dz) for dy, dz in PEERS] + [right, left, core, far])
    links = Links(send_sem, recv_sem)
    own, far_e = me.expert(0, 0), me.expert(0, 1)

    from_far = links.send(w_in, w_out.at[own, me.c], far)
    from_left0 = links.send(w_in, w_out.at[own, me.c], right)
    from_right0 = links.send(w_in, w_out.at[own, me.c], left)
    columns = []
    for dy, dz in PEERS:
        there, device = me.block(dy, dz), me.to(y=dy, zl=dz)
        cols = pl.ds(pl.multiple_of(there * 768, 768), 768)
        columns.append(links.send(tok.at[:, cols], x_out.at[me.q], device))
        columns.append(links.send(og.at[:, cols], og_out.at[me.q], device))
        columns.append(links.send(ids, ids_out.at[me.q], device))
    from_core = [links.send(w_in, w_out.at[own, me.c], core)]
    cols = pl.ds(pl.multiple_of(me.q * 768, 768), 768)
    local = [
        pltpu.make_async_copy(w_in, w_out.at[own, me.c], own_sem.at[0]),
        pltpu.make_async_copy(tok.at[:, cols], x_out.at[me.q], own_sem.at[1]),
        pltpu.make_async_copy(og.at[:, cols], og_out.at[me.q], own_sem.at[2]),
        pltpu.make_async_copy(ids, ids_out.at[me.q], own_sem.at[3]),
    ]
    for copy in local:
        copy.start()

    def pass_on(expert, device, rows=pl.ds(0, 384)):
        piece = w_out.at[expert, me.c, rows, :]
        return links.send(piece, piece, device)

    low, high = pl.ds(0, 192), pl.ds(192, 192)
    from_far.wait_recv()
    from_left1 = pass_on(far_e, right)
    from_right1 = pass_on(far_e, left)
    from_core.append(pass_on(far_e, core))
    halves = []
    for dz, from_left, from_right in ((0, from_left0, from_right0), (1, from_left1, from_right1)):
        from_left.wait_recv()
        halves.append(pass_on(me.expert(3, dz), right, low))
        from_core.append(pass_on(me.expert(3, dz), core))
        from_right.wait_recv()
        halves.append(pass_on(me.expert(1, dz), left, high))
        from_core.append(pass_on(me.expert(1, dz), core))
    for n, half in enumerate(halves):
        half.wait_recv()
        from_core.append(pass_on(me.expert(2, n // 2), core, (low, high)[n % 2]))
    for copy in columns + from_core:
        copy.wait_recv()
    for copy in local:
        copy.wait()
    links.finish()


def spread(tokens, out_grad, ids, w_cat):
    vmem, anywhere = pl.BlockSpec(memory_space=pltpu.VMEM), pl.BlockSpec(memory_space=pl.ANY)
    return pl.pallas_call(
        spread_kernel,
        out_shape=(
            jax.ShapeDtypeStruct((8, 128, 768), BF16),
            jax.ShapeDtypeStruct((8, 128, 768), BF16),
            jax.ShapeDtypeStruct((8, 8, 128), jnp.int32),
            jax.ShapeDtypeStruct((8, 2, 384, 768), BF16),
        ),
        in_specs=[vmem] * 4,
        out_specs=(anywhere,) * 4,
        scratch_shapes=[
            pltpu.SemaphoreType.DMA((SPREAD_COPIES,)),
            pltpu.SemaphoreType.DMA((SPREAD_COPIES,)),
            pltpu.SemaphoreType.DMA((4,)),
        ],
        compiler_params=pltpu.CompilerParams(collective_id=0, has_side_effects=True),
        name="spread",
    )(tokens, out_grad, ids, w_cat)


def activation(pre, weight):
    gate, up, grad_hidden = pre[:, :256], pre[:, 256:512], pre[:, 512:] * weight
    sig = jax.nn.sigmoid(gate)
    silu = gate * sig
    hidden = silu * up * weight
    grad_gate = grad_hidden * up * sig * (1.0 + gate * (1.0 - sig))
    grad_up = grad_hidden * silu
    return grad_gate.astype(BF16), grad_up.astype(BF16), hidden.astype(BF16)


MIDDLE_COPIES = 8 + 4 + 1 + 3 + 2 + 4


def middle_kernel(part, weight, h_out, ra, rb, sa, sb, fl, fr, zs, zr, own, send_sem, recv_sem, own_sem):
    me = Spot()
    right, left, pair = me.to(y=1), me.to(y=3), me.to(zl=1)
    greet([right, left, pair])
    links = Links(send_sem, recv_sem)
    low, high = pl.ds(0, 128), pl.ds(128, 128)

    first_a, first_b, other_b, other_a, last_a, last_b = {}, {}, {}, {}, {}, {}
    for dz in (1, 0):
        first_a[dz] = links.send(part.at[me.block(2, dz), low, :], ra.at[dz], right)
        first_b[dz] = links.send(part.at[me.block(2, dz), high, :], rb.at[dz], left)
    for dz in (1, 0):
        other_b[dz] = links.send(part.at[me.block(1, dz), high, :], fl.at[dz, high, :], right)
        other_a[dz] = links.send(part.at[me.block(3, dz), low, :], fr.at[dz, low, :], left)
    for dz in (1, 0):
        first_a[dz].wait_recv()
        add_rows(sa.at[dz], [part.at[me.block(1, dz), low, :], ra.at[dz]], 128)
        last_a[dz] = links.send(sa.at[dz], fl.at[dz, low, :], right)
        first_b[dz].wait_recv()
        add_rows(sb.at[dz], [part.at[me.block(3, dz), high, :], rb.at[dz]], 128)
        last_b[dz] = links.send(sb.at[dz], fr.at[dz, high, :], left)
    for group in (other_b, other_a, last_a, last_b):
        group[1].wait_recv()
    add_rows(zs, [part.at[me.block(0, 1)], fl.at[1], fr.at[1]], 256)
    cross = links.send(zs, zr, pair)
    for group in (other_b, other_a, last_a, last_b):
        group[0].wait_recv()
    cross.wait_recv()

    @pl.loop(0, 16)
    def _(i):
        at = pl.ds(pl.multiple_of(i * 16, 16), 16)
        pre = part[me.block(0, 0), at, :].astype(F32) + zr[at, :].astype(F32)
        pre = pre + fl[0, at, :].astype(F32) + fr[0, at, :].astype(F32)
        own[at, :256], own[at, 256:512], own[at, 512:] = activation(pre, weight[at, :])

    mine = pltpu.make_async_copy(own, h_out.at[me.q], own_sem)
    mine.start()
    from_pair = links.send(own, h_out.at[me.q], pair)
    from_left0 = links.send(own, h_out.at[me.q], right)
    from_right0 = links.send(own, h_out.at[me.q], left)

    def pass_on(block, device, rows=pl.ds(0, 256)):
        piece = h_out.at[block, rows, :]
        return links.send(piece, piece, device)

    from_pair.wait_recv()
    from_left1 = pass_on(me.block(0, 1), right)
    from_right1 = pass_on(me.block(0, 1), left)
    halves = []
    for dz, from_left, from_right in ((0, from_left0, from_right0), (1, from_left1, from_right1)):
        from_left.wait_recv()
        halves.append(pass_on(me.block(3, dz), right, low))
        from_right.wait_recv()
        halves.append(pass_on(me.block(1, dz), left, high))
    for half in halves:
        half.wait_recv()
    mine.wait()
    links.finish()


def middle(part, weight):
    vmem, anywhere = pl.BlockSpec(memory_space=pltpu.VMEM), pl.BlockSpec(memory_space=pl.ANY)
    half, full = pltpu.VMEM((2, 128, 768), BF16), pltpu.VMEM((2, 256, 768), BF16)
    one = pltpu.VMEM((256, 768), BF16)
    return pl.pallas_call(
        middle_kernel,
        out_shape=jax.ShapeDtypeStruct((8, 256, 768), BF16),
        in_specs=[vmem] * 2,
        out_specs=anywhere,
        scratch_shapes=[half] * 4 + [full] * 2 + [one] * 3 + [
            pltpu.SemaphoreType.DMA((MIDDLE_COPIES,)),
            pltpu.SemaphoreType.DMA((MIDDLE_COPIES,)),
            pltpu.SemaphoreType.DMA,
        ],
        compiler_params=pltpu.CompilerParams(collective_id=1, has_side_effects=True),
        name="middle",
    )(part, weight)


FINISH_COPIES = 7 + 8 + 4 + 4 + 4 + 1
ORDER = ((2, 1), (1, 1), (3, 1), (2, 0), (1, 0), (3, 0), (0, 1), (0, 0))


def finish_kernel(
    x, og, ids, h, w, d_out, g_out,
    xt, ogt, w_all, he, g, cr, dx, a2, ra, rb, sa, sb, oa, ob, fl, fr, zs, zr,
    send_sem, recv_sem, w_sem, own_sem,
):
    me = Spot()
    right, left, core, far = me.to(x=1), me.to(x=3), me.to(c=1), me.to(zh=1)
    loads = [pltpu.make_async_copy(w.at[e], w_all.at[e], w_sem.at[e]) for e in range(8)]
    for load in loads:
        load.start()
    for q in range(8):
        xt[:, q * 128 : q * 128 + 128] = jnp.transpose(x[q])
        ogt[:, q * 128 : q * 128 + 128] = jnp.transpose(og[q])
    greet([me.to(y=dy, zl=dz) for dy, dz in PEERS] + [right, left, core, far])
    links = Links(send_sem, recv_sem)
    low, high = pl.ds(0, 192), pl.ds(192, 192)
    mine, others = me.c, 1 - me.c
    swapped, first_a, first_b, other_b, other_a, last_a, last_b = {}, {}, {}, {}, {}, {}, {}

    def product(step, dz):
        e = me.expert(step, dz)

        @pl.loop(0, 32)
        def _(i):
            at = pl.ds(pl.multiple_of(i * 32, 32), 32)
            q, row = i // 4, pl.multiple_of(i % 4 * 32, 32)
            m0 = (ids[at, 0:1] == e).astype(F32)
            m1 = (ids[at, 1:2] == e).astype(F32)
            h0 = h[q, pl.ds(row, 32), :].astype(F32)
            h1 = h[q, pl.ds(row + 128, 32), :].astype(F32)
            he[e, at, :] = (h0 * m0 + h1 * m1).astype(BF16)

        for n, left_t in ((0, xt), (1, xt), (2, ogt)):
            cols = slice(n * 256, n * 256 + 256)
            out = jnp.dot(left_t[...], he[e, :, cols], preferred_element_type=F32).astype(BF16)
            g[e, 0, :, cols] = out[:384]
            g[e, 1, :, cols] = out[384:]
        swapped[step, dz] = links.send(g.at[e, others], cr.at[e], core)

    def start_far(dz):
        e = me.expert(2, dz)
        swapped[2, dz].wait_recv()
        add_rows(a2.at[dz], [g.at[e, mine], cr.at[e]], 384)
        first_a[dz] = links.send(a2.at[dz, low, :], ra.at[dz], right)
        first_b[dz] = links.send(a2.at[dz, high, :], rb.at[dz], left)

    def start_near(dz):
        e = me.expert(1, dz)
        swapped[1, dz].wait_recv()
        add_rows(ob.at[dz], [g.at[e, mine, high, :], cr.at[e, high, :]], 192)
        other_b[dz] = links.send(ob.at[dz], fl.at[dz, high, :], right)
        e = me.expert(3, dz)
        swapped[3, dz].wait_recv()
        add_rows(oa.at[dz], [g.at[e, mine, low, :], cr.at[e, low, :]], 192)
        other_a[dz] = links.send(oa.at[dz], fr.at[dz, low, :], left)

    def relay(dz):
        e = me.expert(1, dz)
        first_a[dz].wait_recv()
        add_rows(sa.at[dz], [g.at[e, mine, low, :], cr.at[e, low, :], ra.at[dz]], 192)
        last_a[dz] = links.send(sa.at[dz], fl.at[dz, low, :], right)
        e = me.expert(3, dz)
        first_b[dz].wait_recv()
        add_rows(sb.at[dz], [g.at[e, mine, high, :], cr.at[e, high, :], rb.at[dz]], 192)
        last_b[dz] = links.send(sb.at[dz], fr.at[dz, high, :], left)

    def token_part(n):
        cols = slice(n * 256, n * 256 + 256)
        total = None
        for e in range(8):
            part = lax.dot_general(
                he[e, :, :512], w_all[e, cols, :512], (((1,), (1,)), ((), ())), preferred_element_type=F32
            )
            total = part if total is None else total + part
        for q in range(8):
            dx[q, :, cols] = total[q * 128 : q * 128 + 128].astype(BF16)

    product(2, 1)
    product(1, 1)
    start_far(1)
    product(3, 1)
    product(2, 0)
    start_near(1)
    product(1, 0)
    start_far(0)
    product(3, 0)
    product(0, 1)
    start_near(0)
    relay(1)
    product(0, 0)
    for load in loads:
        load.wait()
    token_part(0)
    token_part(1)
    token_part(2)
    back = []
    cols = pl.ds(pl.multiple_of(me.q * 768, 768), 768)
    for dy, dz in PEERS:
        back.append(links.send(dx.at[me.block(dy, dz)], d_out.at[:, cols], me.to(y=dy, zl=dz)))
    keep = pltpu.make_async_copy(dx.at[me.q], d_out.at[:, cols], own_sem)
    keep.start()
    relay(0)
    for group in (other_b, other_a, last_a, last_b):
        group[1].wait_recv()
    e = me.expert(0, 1)
    swapped[0, 1].wait_recv()
    add_rows(zs, [g.at[e, mine], cr.at[e], fl.at[1], fr.at[1]], 384)
    cross = links.send(zs, zr, far)
    for group in (other_b, other_a, last_a, last_b):
        group[0].wait_recv()
    swapped[0, 0].wait_recv()
    cross.wait_recv()
    e = me.expert(0, 0)
    add_rows(g_out, [g.at[e, mine], cr.at[e], fl.at[0], fr.at[0], zr], 384)
    for copy in back:
        copy.wait_recv()
    keep.wait()
    links.finish()


def finish(x, og, ids, h, w):
    vmem, anywhere = pl.BlockSpec(memory_space=pltpu.VMEM), pl.BlockSpec(memory_space=pl.ANY)
    half, full = pltpu.VMEM((2, 192, 768), BF16), pltpu.VMEM((2, 384, 768), BF16)
    one = pltpu.VMEM((384, 768), BF16)
    return pl.pallas_call(
        finish_kernel,
        out_shape=(
            jax.ShapeDtypeStruct((128, 6144), BF16),
            jax.ShapeDtypeStruct((384, 768), F32),
        ),
        in_specs=[vmem] * 4 + [anywhere],
        out_specs=(anywhere, vmem),
        scratch_shapes=[
            pltpu.VMEM((768, 1024), BF16),
            pltpu.VMEM((768, 1024), BF16),
            pltpu.VMEM((8, 768, 768), BF16),
            pltpu.VMEM((8, 1024, 768), BF16),
            pltpu.VMEM((8, 2, 384, 768), BF16),
            pltpu.VMEM((8, 384, 768), BF16),
            pltpu.VMEM((8, 128, 768), BF16),
        ]
        + [full] + [half] * 6 + [full] * 2 + [one] * 2
        + [
            pltpu.SemaphoreType.DMA((FINISH_COPIES,)),
            pltpu.SemaphoreType.DMA((FINISH_COPIES,)),
            pltpu.SemaphoreType.DMA((8,)),
            pltpu.SemaphoreType.DMA,
        ],
        compiler_params=pltpu.CompilerParams(collective_id=2, has_side_effects=True, vmem_limit_bytes=60 << 20),
        name="finish",
    )(x, og, ids, h, w)


def partial_pre(x, og, ids_all, w):
    total = [jnp.zeros((1024, 768), F32) for _ in range(2)]
    for e in range(8):
        y = jnp.concatenate(
            [
                jnp.dot(x, w[e, :, :512], preferred_element_type=F32),
                jnp.dot(og, w[e, :, 512:], preferred_element_type=F32),
            ],
            axis=1,
        )
        for k in range(2):
            total[k] = jnp.where(ids_all[:, k : k + 1] == e, y, total[k])
    both = jnp.stack([t.reshape(8, 128, 768) for t in total], axis=1)
    return both.reshape(8, 256, 768).astype(BF16)


def shards(tokens, out_grad, expert_ids, route_weight, w_gate, w_up, w_down):
    w_cat = jnp.concatenate([w_gate[0], w_up[0], jnp.transpose(w_down[0])], axis=1)
    ids = jnp.zeros((8, 128), jnp.int32).at[:2].set(jnp.transpose(expert_ids))
    x, og, ids_all, w = spread(tokens, out_grad, ids, w_cat)
    w = w.reshape(8, 768, 768)
    ids_all = jnp.transpose(ids_all[:, :2], (0, 2, 1)).reshape(1024, 2)
    part = partial_pre(x.reshape(1024, 768), og.reshape(1024, 768), ids_all, w)
    h = middle(part, jnp.transpose(route_weight).reshape(256, 1))
    d_tokens, g = finish(x, og, ids_all, h, w)
    return d_tokens, g[None, :, :256], g[None, :, 256:512], jnp.transpose(g[:, 512:])[None]


def solution(mesh):
    in_specs = (
        P(("dp", "ep"), None),
        P(("dp", "ep"), None),
        P(("dp", "ep"), None),
        P(("dp", "ep"), None),
        P("ep", "dp", None),
        P("ep", "dp", None),
        P("ep", None, "dp"),
    )
    out_specs = (
        P(("dp", "ep"), None),
        P("ep", "dp", None),
        P("ep", "dp", None),
        P("ep", None, "dp"),
    )
    return jax.shard_map(shards, mesh=mesh, in_specs=in_specs, out_specs=out_specs, check_vma=False)
```

profile of v0, /device:TPU:1, one launch (start us, length us, event | category | flops | bytes accessed | tf_op | source)
XLA Modules:
  0.0 286.2 jit_solution(8295214397177511081)
XLA Ops:
  0.6 0.0 copy-start.19
  0.6 1.1 copy.15
  1.7 1.9 pad_maximum_fusion.9.w_in
  3.6 0.0 copy-done.19
  3.6 0.6 scatter.4.ids
  4.2 81.8 %spread.1 = (bf16[8,128,768]{2,1,0:T(8,128)(2,1)}, bf16[8,128,768]{2,1,0:T(8,128)(2,1)}, s32[8,8,128]{2,1,0:T(8,128)}, bf16[8,2,384,768]{3,2,1,0:T(8,128)(2,1)}) custom-call(bf16[128,6144]{1,0:T(8,128)(2,1)} %tok.1, bf16[128,6144]{1,0:T(8,128)(2,1)} %og.1, s32[8,128]{1,0:T(8,128)} %scatter.4.ids, bf16[384,768]{1,0:T(8,128)(2,1)} %pad_maximum_fusion.9.w_in), custom_call_target="tpu_custom_call" | custom-call | tf_op jit(solution)/shard_map/spread/pallas_call | solution.py:134
  86.0 2.7 convolution_bitcast_fusion.7
  88.7 2.7 convolution_bitcast_fusion.15
  91.4 2.7 convolution_bitcast_fusion.6
  94.1 0.0 copy-done
  94.1 0.0 copy-done.17
  94.1 0.0 copy-start.16
  94.1 1.4 convolution_bitcast_fusion.14
  95.5 2.0 convolution_bitcast_fusion.5
  97.5 1.4 convolution_bitcast_fusion.13
  98.9 2.0 convolution_bitcast_fusion.4
  100.8 1.4 convolution_bitcast_fusion.12
  102.2 1.9 convolution_bitcast_fusion.3
  104.2 1.4 convolution_bitcast_fusion.11
  105.5 2.0 convolution_bitcast_fusion.2
  107.6 1.4 convolution_bitcast_fusion.10
  109.0 1.9 convolution_bitcast_fusion.1
  110.9 1.4 convolution_bitcast_fusion.9
  112.3 1.9 convolution_bitcast_fusion
  114.3 1.4 convolution_bitcast_fusion.8
  115.6 0.8 slice_bitcast_fusion.35
  116.4 0.2 copy.16
  116.7 2.6 compare_reduce_fusion.15
  119.3 0.0 copy-start.7
  119.3 0.0 copy-start.8
  119.3 0.0 copy-start.9
  119.3 0.0 copy-start.10
  119.3 0.0 copy-start.11
  119.3 0.0 copy-start.12
  119.3 0.0 copy-start.13
  119.3 0.0 copy-start.14
  119.4 8.0 %select_convert_fusion.1 = bf16[8,1,128,768]{3,2,0,1:T(8,128)(2,1)S(1)} fusion(bf16[8,1,128,256]{3,2,0,1:T(8,128)(2,1)} %convolution_bitcast_fusion.8, bf16[8,1,128,512]{3,2,0,1:T(8,128)(2,1)} %convolution_bitcast_fusion, bf16[8,1,128,256]{3,2,0,1:T(8,128)(2,1)} %convolution_bitcast_fusion.9, bf16[8,1,128,512]{3,2,0,1:T(8,128)(2,1)} %convolution_bitcast_fusion.1, ...), kind=kLoop, calls=%fused_computation.10 | loop fusion | flops 31457280 | bytes 14163968 | tf_op jit(solution)/shard_map/convert
  127.5 3.2 %select_convert_fusion = bf16[8,1,128,768]{3,2,0,1:T(8,128)(2,1)S(1)} fusion(bf16[8,1,128,256]{3,2,0,1:T(8,128)(2,1)S(1)} %copy-done.14, bf16[8,1,128,512]{3,2,0,1:T(8,128)(2,1)S(1)} %copy-done.7, bf16[8,1,128,256]{3,2,0,1:T(8,128)(2,1)S(1)} %copy-done.13, bf16[8,1,128,512]{3,2,0,1:T(8,128)(2,1)S(1)} %copy-done.6, bf16[8,1,128,256]{3,2,0,1:T(8,128)(2,1)S(1)} %copy-done.12, ...), kind=kLoop, calls=%fused_computation.9 | loop fusion | flops 31457280 | bytes 14163968 | tf_op jit(solution)/shard_map/convert.1
  130.7 0.3 pad_maximum_fusion.8
  131.0 0.0 copy-start.18
  131.0 2.0 copy.17
  133.0 0.8 copy.18.weight
  133.8 61.8 %middle.1.h = bf16[8,256,768]{2,1,0:T(8,128)(2,1)} custom-call(bf16[8,256,768]{2,1,0:T(8,128)(2,1)} %bitcast.150, f32[256,1]{1,0:T(8,128)} %copy.18.weight), custom_call_target="tpu_custom_call" | custom-call | tf_op jit(solution)/shard_map/middle/pallas_call | solution.py:232
  195.6 86.2 %finish.1 = (bf16[128,6144]{1,0:T(8,128)(2,1)}, f32[384,768]{1,0:T(8,128)}) custom-call(bf16[8,128,768]{2,1,0:T(8,128)(2,1)} %get-tuple-element.22.x, bf16[8,128,768]{2,1,0:T(8,128)(2,1)} %get-tuple-element.23.og, s32[1024,2]{1,0:T(8,128)} %bitcast.169, bf16[8,256,768]{2,1,0:T(8,128)(2,1)} %middle.1.h, bf16[8,768,768]{2,1,0:T(8,128)(2,1)} %bitcast.154), custom_call_target="tpu_custom_call" | custom-call | tf_op jit(solution)/shard_map/finish/pallas_call | solution.py:375
  281.8 2.3 slice_bitcast_fusion.32
  284.1 0.9 copy.19
  285.0 0.0 copy-done.15
  285.0 1.1 copy.21
  (25 shorter events, 0.1 us)
Async XLA Ops:
  0.6 3.0 %copy-start.19 = (s32[128,2]{0,1:T(2,128)S(1)}, s32[128,2]{0,1:T(2,128)}, u32[]{:S(2)}) copy-start(s32[128,2]{0,1:T(2,128)} %param.11) | copy-start | bytes 3076
  86.0 8.1 %copy-start = (bf16[8,2,384,768]{3,2,1,0:T(8,128)(2,1)S(1)}, bf16[8,2,384,768]{3,2,1,0:T(8,128)(2,1)}, u32[]{:S(2)}) copy-start(bf16[8,2,384,768]{3,2,1,0:T(8,128)(2,1)} %get-tuple-element.25) | copy-start | bytes 28311556
  91.4 2.7 copy-start.17
  94.1 1.4 copy-start.16
  116.6 10.7 %copy-start.1 = (s32[8,128,2]{2,1,0:T(8,128)}, s32[8,128,2]{2,1,0:T(8,128)S(1)}, u32[]{:S(2)}) copy-start(s32[8,128,2]{2,1,0:T(8,128)S(1)} %copy.16) | copy-start | bytes 24580
  116.6 2.6 copy-start.2
  119.2 8.1 %copy-start.3 = (bf16[8,1,128,512]{3,2,0,1:T(8,128)(2,1)S(1)}, bf16[8,1,128,512]{3,2,0,1:T(8,128)(2,1)}, u32[]{:S(2)}) copy-start(bf16[8,1,128,512]{3,2,0,1:T(8,128)(2,1)} %convolution_bitcast_fusion.4) | copy-start | bytes 3145732
  119.2 8.1 %copy-start.4 = (bf16[8,1,128,512]{3,2,0,1:T(8,128)(2,1)S(1)}, bf16[8,1,128,512]{3,2,0,1:T(8,128)(2,1)}, u32[]{:S(2)}) copy-start(bf16[8,1,128,512]{3,2,0,1:T(8,128)(2,1)} %convolution_bitcast_fusion.3) | copy-start | bytes 3145732
  119.3 8.1 %copy-start.5 = (bf16[8,1,128,512]{3,2,0,1:T(8,128)(2,1)S(1)}, bf16[8,1,128,512]{3,2,0,1:T(8,128)(2,1)}, u32[]{:S(2)}) copy-start(bf16[8,1,128,512]{3,2,0,1:T(8,128)(2,1)} %convolution_bitcast_fusion.2) | copy-start | bytes 3145732
  119.3 8.1 %copy-start.6 = (bf16[8,1,128,512]{3,2,0,1:T(8,128)(2,1)S(1)}, bf16[8,1,128,512]{3,2,0,1:T(8,128)(2,1)}, u32[]{:S(2)}) copy-start(bf16[8,1,128,512]{3,2,0,1:T(8,128)(2,1)} %convolution_bitcast_fusion.1) | copy-start | bytes 3145732
  119.3 8.1 %copy-start.7 = (bf16[8,1,128,512]{3,2,0,1:T(8,128)(2,1)S(1)}, bf16[8,1,128,512]{3,2,0,1:T(8,128)(2,1)}, u32[]{:S(2)}) copy-start(bf16[8,1,128,512]{3,2,0,1:T(8,128)(2,1)} %convolution_bitcast_fusion) | copy-start | bytes 3145732
  119.3 8.1 %copy-start.8 = (bf16[8,1,128,256]{3,2,0,1:T(8,128)(2,1)S(1)}, bf16[8,1,128,256]{3,2,0,1:T(8,128)(2,1)}, u32[]{:S(2)}) copy-start(bf16[8,1,128,256]{3,2,0,1:T(8,128)(2,1)} %convolution_bitcast_fusion.14) | copy-start | bytes 1572868
  119.3 8.1 %copy-start.9 = (bf16[8,1,128,256]{3,2,0,1:T(8,128)(2,1)S(1)}, bf16[8,1,128,256]{3,2,0,1:T(8,128)(2,1)}, u32[]{:S(2)}) copy-start(bf16[8,1,128,256]{3,2,0,1:T(8,128)(2,1)} %convolution_bitcast_fusion.13) | copy-start | bytes 1572868
  119.3 8.1 %copy-start.10 = (bf16[8,1,128,256]{3,2,0,1:T(8,128)(2,1)S(1)}, bf16[8,1,128,256]{3,2,0,1:T(8,128)(2,1)}, u32[]{:S(2)}) copy-start(bf16[8,1,128,256]{3,2,0,1:T(8,128)(2,1)} %convolution_bitcast_fusion.12) | copy-start | bytes 1572868
  119.3 8.1 %copy-start.11 = (bf16[8,1,128,256]{3,2,0,1:T(8,128)(2,1)S(1)}, bf16[8,1,128,256]{3,2,0,1:T(8,128)(2,1)}, u32[]{:S(2)}) copy-start(bf16[8,1,128,256]{3,2,0,1:T(8,128)(2,1)} %convolution_bitcast_fusion.11) | copy-start | bytes 1572868
  119.3 8.1 %copy-start.12 = (bf16[8,1,128,256]{3,2,0,1:T(8,128)(2,1)S(1)}, bf16[8,1,128,256]{3,2,0,1:T(8,128)(2,1)}, u32[]{:S(2)}) copy-start(bf16[8,1,128,256]{3,2,0,1:T(8,128)(2,1)} %convolution_bitcast_fusion.10) | copy-start | bytes 1572868
  119.3 8.1 %copy-start.13 = (bf16[8,1,128,256]{3,2,0,1:T(8,128)(2,1)S(1)}, bf16[8,1,128,256]{3,2,0,1:T(8,128)(2,1)}, u32[]{:S(2)}) copy-start(bf16[8,1,128,256]{3,2,0,1:T(8,128)(2,1)} %convolution_bitcast_fusion.9) | copy-start | bytes 1572868
  119.3 8.1 %copy-start.14 = (bf16[8,1,128,256]{3,2,0,1:T(8,128)(2,1)S(1)}, bf16[8,1,128,256]{3,2,0,1:T(8,128)(2,1)}, u32[]{:S(2)}) copy-start(bf16[8,1,128,256]{3,2,0,1:T(8,128)(2,1)} %convolution_bitcast_fusion.8) | copy-start | bytes 1572868
  131.0 2.0 copy-start.18
  281.8 3.2 %copy-start.15 = (bf16[128,6144]{1,0:T(8,128)(2,1)S(1)}, bf16[128,6144]{1,0:T(8,128)(2,1)}, u32[]{:S(2)}) copy-start(bf16[128,6144]{1,0:T(8,128)(2,1)} %get-tuple-element.59) | copy-start | bytes 4718596
where the time goes:
time: 286 us
  Pallas kernels  230 us (80%)
  matrix products  29.6 us (10%)
  other arithmetic  15.9 us (6%)
  local copies, waits for them, and re-layouts  9.86 us (3%)
    pallas_call x1, Pallas kernels, finish(): pl.pallas_call(finish_kernel, out_shape=(jax.ShapeDtypeStruct((128, 6144)...  86.2 us
    pallas_call x1, Pallas kernels, spread(): pl.pallas_call(spread_kernel, out_shape=(jax.ShapeDtypeStruct((8, 128, 76...  81.8 us
    pallas_call x1, Pallas kernels, middle(): pl.pallas_call(middle_kernel, out_shape=jax.ShapeDtypeStruct((8, 256, 768...  61.8 us
    dot_general x8, matrix products, partial_pre(): jnp.dot(x, w[e, :, :512], preferred_element_type=F32)  17.2 us
    dot_general x8, matrix products, partial_pre(): jnp.dot(og, w[e, :, 512:], preferred_element_type=F32)  12.4 us
    another operation x2, other arithmetic  11.2 us

commit v1 on v0

--- a/solution.py
+++ b/solution.py
@@ -17,14 +17,18 @@
         dp, ep = lax.axis_index("dp"), lax.axis_index("ep")
         self.y, self.zl, self.c = dp // 4, (dp // 2) % 2, dp % 2
         self.zh, self.x = ep // 4, ep % 4
-        self.q = dp // 2
+        self.b = self.block(0, 0)
 
     def to(self, y=0, zl=0, c=0, zh=0, x=0):
         dp = (self.y + y) % 4 * 4 + (self.zl + zl) % 2 * 2 + (self.c + c) % 2
         return (dp, (self.zh + zh) % 2 * 4 + (self.x + x) % 4)
 
     def block(self, y, zl):
-        return (self.y + y) % 4 * 2 + (self.zl + zl) % 2
+        return (self.zl + zl) % 2 * 4 + (self.y + y) % 4
+
+    def columns(self, y, zl, width=768, offset=0):
+        start = ((self.y + y) % 4 * 2 + (self.zl + zl) % 2) * 768 + offset
+        return pl.ds(pl.multiple_of(start, 128), width)
 
     def expert(self, x, zh):
         return (self.zh + zh) % 2 * 4 + (self.x + x) % 4
@@ -50,6 +54,7 @@
         return copy
 
     def finish(self):
+        assert self.count == self.send_sem.shape[0]
         for copy in self.sent:
             copy.wait_send()
 
@@ -71,82 +76,212 @@
         dst[at, :] = total.astype(dst.dtype)
 
 
-SPREAD_COPIES = 21 + 1 + 2 + 1 + 3 + 6 + 6 + 4
-
-
-def spread_kernel(tok, og, ids, w_in, x_out, og_out, ids_out, w_out, send_sem, recv_sem, own_sem):
+SPREAD_COPIES = 19 + 24 + 7
+
+
+def spread_kernel(
+    tok, og, ids, w_in, part, xt, ogt, idc, w_out,
+    x, g, ids_in, w, z_tok, z_og, l_tok, r_og, send_sem, recv_sem, own_sem, w_sem,
+):
     me = Spot()
-    right, left, core, far = me.to(x=1), me.to(x=3), me.to(c=1), me.to(zh=1)
+    right, left, up, down = me.to(x=1), me.to(x=3), me.to(y=1), me.to(y=3)
+    core, far, pair = me.to(c=1), me.to(zh=1), me.to(zl=1)
     greet([me.to(y=dy, zl=dz) for dy, dz in PEERS] + [right, left, core, far])
     links = Links(send_sem, recv_sem)
     own, far_e = me.expert(0, 0), me.expert(0, 1)
 
-    from_far = links.send(w_in, w_out.at[own, me.c], far)
-    from_left0 = links.send(w_in, w_out.at[own, me.c], right)
-    from_right0 = links.send(w_in, w_out.at[own, me.c], left)
-    columns = []
-    for dy, dz in PEERS:
-        there, device = me.block(dy, dz), me.to(y=dy, zl=dz)
-        cols = pl.ds(pl.multiple_of(there * 768, 768), 768)
-        columns.append(links.send(tok.at[:, cols], x_out.at[me.q], device))
-        columns.append(links.send(og.at[:, cols], og_out.at[me.q], device))
-        columns.append(links.send(ids, ids_out.at[me.q], device))
-    from_core = [links.send(w_in, w_out.at[own, me.c], core)]
-    cols = pl.ds(pl.multiple_of(me.q * 768, 768), 768)
+    from_far = links.send(w_in, w.at[own, me.c], far)
+    from_left0 = links.send(w_in, w.at[own, me.c], right)
+    from_right0 = links.send(w_in, w.at[own, me.c], left)
+    from_core = {(0, 0): [links.send(w_in, w.at[own, me.c], core)]}
+
+    def cut(array, y, zl):
+        return array.at[:, me.columns(y, zl)]
+
+    plane = [
+        links.send(cut(tok, 2, 0), l_tok.at[0], up),
+        links.send(cut(og, 2, 0), r_og.at[0], down),
+    ]
+    z_in = {}
+    z_in[2, 0] = links.send(cut(tok, 2, 1), z_tok.at[2], pair)
+    z_in[2, 1] = links.send(cut(og, 2, 1), z_og.at[2], pair)
+    near = []
+    for y, device in ((1, up), (3, down)):
+        near.append(links.send(cut(tok, y, 0), x.at[me.b], device))
+        near.append(links.send(cut(og, y, 0), g.at[me.b], device))
+    for y in (1, 3):
+        z_in[y, 0] = links.send(cut(tok, y, 1), z_tok.at[y], pair)
+        z_in[y, 1] = links.send(cut(og, y, 1), z_og.at[y], pair)
+    z_in[0, 0] = links.send(cut(tok, 0, 1), x.at[me.b], pair)
+    z_in[0, 1] = links.send(cut(og, 0, 1), g.at[me.b], pair)
+    names = [links.send(ids, ids_in.at[me.b], me.to(y=dy, zl=dz)) for dy, dz in PEERS]
     local = [
-        pltpu.make_async_copy(w_in, w_out.at[own, me.c], own_sem.at[0]),
-        pltpu.make_async_copy(tok.at[:, cols], x_out.at[me.q], own_sem.at[1]),
-        pltpu.make_async_copy(og.at[:, cols], og_out.at[me.q], own_sem.at[2]),
-        pltpu.make_async_copy(ids, ids_out.at[me.q], own_sem.at[3]),
+        pltpu.make_async_copy(w_in, w.at[own, me.c], own_sem.at[0]),
+        pltpu.make_async_copy(cut(tok, 0, 0), x.at[me.b], own_sem.at[1]),
+        pltpu.make_async_copy(cut(og, 0, 0), g.at[me.b], own_sem.at[2]),
+        pltpu.make_async_copy(ids, ids_in.at[me.b], own_sem.at[3]),
     ]
     for copy in local:
         copy.start()
 
+    @pl.loop(0, 64)
+    def _(i):
+        part[i // 8, pl.ds(pl.multiple_of(i % 8 * 32, 32), 32), :] = jnp.zeros((32, 768), BF16)
+
     def pass_on(expert, device, rows=pl.ds(0, 384)):
-        piece = w_out.at[expert, me.c, rows, :]
+        piece = w.at[expert, me.c, rows, :]
         return links.send(piece, piece, device)
 
     low, high = pl.ds(0, 192), pl.ds(192, 192)
+    across, ends = [], []
+    z_in[2, 0].wait_recv()
+    across.append(links.send(z_tok.at[2], l_tok.at[1], up))
+    plane[0].wait_recv()
+    ends.append(links.send(l_tok.at[0], x.at[me.block(3, 0)], up))
+    z_in[2, 1].wait_recv()
+    across.append(links.send(z_og.at[2], r_og.at[1], down))
+    plane[1].wait_recv()
+    ends.append(links.send(r_og.at[0], g.at[me.block(1, 0)], down))
+    halves = {0: [], 1: []}
+
+    def sideways(dz, from_left, from_right):
+        from_left.wait_recv()
+        halves[dz].append(pass_on(me.expert(3, dz), right, low))
+        from_core[3, dz] = [pass_on(me.expert(3, dz), core)]
+        from_right.wait_recv()
+        halves[dz].append(pass_on(me.expert(1, dz), left, high))
+        from_core[1, dz] = [pass_on(me.expert(1, dz), core)]
+
+    sideways(0, from_left0, from_right0)
+    late = []
+
+    def partner(y, device):
+        z_in[y, 0].wait_recv()
+        late.append(links.send(z_tok.at[y], x.at[me.block(0, 1)], device))
+        z_in[y, 1].wait_recv()
+        late.append(links.send(z_og.at[y], g.at[me.block(0, 1)], device))
+
+    partner(1, up)
     from_far.wait_recv()
     from_left1 = pass_on(far_e, right)
     from_right1 = pass_on(far_e, left)
-    from_core.append(pass_on(far_e, core))
-    halves = []
-    for dz, from_left, from_right in ((0, from_left0, from_right0), (1, from_left1, from_right1)):
-        from_left.wait_recv()
-        halves.append(pass_on(me.expert(3, dz), right, low))
-        from_core.append(pass_on(me.expert(3, dz), core))
-        from_right.wait_recv()
-        halves.append(pass_on(me.expert(1, dz), left, high))
-        from_core.append(pass_on(me.expert(1, dz), core))
-    for n, half in enumerate(halves):
-        half.wait_recv()
-        from_core.append(pass_on(me.expert(2, n // 2), core, (low, high)[n % 2]))
-    for copy in columns + from_core:
+    from_core[0, 1] = [pass_on(far_e, core)]
+    partner(3, down)
+    across[0].wait_recv()
+    late.append(links.send(l_tok.at[1], x.at[me.block(3, 1)], up))
+    across[1].wait_recv()
+    late.append(links.send(r_og.at[1], g.at[me.block(1, 1)], down))
+
+    def second(dz):
+        from_core[2, dz] = []
+        for n, half in enumerate(halves[dz]):
+            half.wait_recv()
+            from_core[2, dz].append(pass_on(me.expert(2, dz), core, (low, high)[n]))
+
+    def turn(dz):
+        for y in range(4):
+            b = me.block(y, dz)
+            at = pl.ds(pl.multiple_of(b * 128, 128), 128)
+            xt[:, at] = jnp.transpose(x[b])
+            ogt[:, at] = jnp.transpose(g[b])
+            idc[at, :] = jnp.transpose(ids_in[b])
+
+    def keep(step, dz):
+        for copy in from_core[step, dz]:
+            copy.wait_recv()
+        e = me.expert(step, dz)
+        pltpu.make_async_copy(w.at[e], w_out.at[e], w_sem.at[e]).start()
+
+    def product(e, dz):
+        plane_at = pl.multiple_of((me.zl + dz) % 2 * 4, 4)
+        for n, source in ((0, x), (1, x), (2, g)):
+            cols = slice(n * 256, n * 256 + 256)
+            rows = source[pl.ds(plane_at, 4)].reshape(512, 768)
+            out = jnp.dot(rows, w[e, :, :, cols].reshape(768, 256), preferred_element_type=F32)
+            for y in range(4):
+                names_at = pl.ds(pl.multiple_of((plane_at + y) * 128, 128), 128)
+                for k in range(2):
+                    here = part.at[plane_at + y, k * 128 : k * 128 + 128, cols]
+                    chosen = idc[names_at, k : k + 1] == e
+                    old = here[...].astype(F32)
+                    here[...] = jnp.where(chosen, out[y * 128 : y * 128 + 128], old).astype(BF16)
+
+    def first_six(i):
+        g2 = i // 2
+        step = (g2 + 1) // 2 * (1 + 2 * (i % 2))
+        return me.expert(step, (1 - (g2 + 1) // 2) * (i % 2) + g2 // 2)
+
+    for copy in near + ends + names:
         copy.wait_recv()
     for copy in local:
         copy.wait()
+    turn(0)
+    for step, dz in ((0, 0), (0, 1), (1, 0), (3, 0)):
+        keep(step, dz)
+
+    @pl.loop(0, 4)
+    def _(i):
+        product(first_six(i), 0)
+
+    second(0)
+    sideways(1, from_left1, from_right1)
+    keep(1, 1)
+    keep(3, 1)
+
+    @pl.loop(4, 6)
+    def _(i):
+        product(first_six(i), 0)
+
+    second(1)
+    for copy in [z_in[0, 0], z_in[0, 1]] + late:
+        copy.wait_recv()
+    turn(1)
+
+    @pl.loop(0, 6)
+    def _(i):
+        product(first_six(i), 1)
+
+    keep(2, 0)
+    keep(2, 1)
+
+    @pl.loop(0, 4)
+    def _(i):
+        product(me.expert(2, i % 2), i // 2)
+
     links.finish()
+    for e in range(8):
+        pltpu.make_async_copy(w.at[e], w_out.at[e], w_sem.at[e]).wait()
 
 
 def spread(tokens, out_grad, ids, w_cat):
     vmem, anywhere = pl.BlockSpec(memory_space=pltpu.VMEM), pl.BlockSpec(memory_space=pl.ANY)
+    blocks = lambda n: pltpu.VMEM((n, 128, 768), BF16)
     return pl.pallas_call(
         spread_kernel,
         out_shape=(
-            jax.ShapeDtypeStruct((8, 128, 768), BF16),
-            jax.ShapeDtypeStruct((8, 128, 768), BF16),
-            jax.ShapeDtypeStruct((8, 8, 128), jnp.int32),
+            jax.ShapeDtypeStruct((8, 256, 768), BF16),
+            jax.ShapeDtypeStruct((768, 1024), BF16),
+            jax.ShapeDtypeStruct((768, 1024), BF16),
+            jax.ShapeDtypeStruct((1024, 8), jnp.int32),
             jax.ShapeDtypeStruct((8, 2, 384, 768), BF16),
         ),
         in_specs=[vmem] * 4,
-        out_specs=(anywhere,) * 4,
+        out_specs=(vmem,) * 4 + (anywhere,),
         scratch_shapes=[
+            blocks(8),
+            blocks(8),
+            pltpu.VMEM((8, 8, 128), jnp.int32),
+            pltpu.VMEM((8, 2, 384, 768), BF16),
+            blocks(4),
+            blocks(4),
+            blocks(2),
+            blocks(2),
             pltpu.SemaphoreType.DMA((SPREAD_COPIES,)),
             pltpu.SemaphoreType.DMA((SPREAD_COPIES,)),
             pltpu.SemaphoreType.DMA((4,)),
+            pltpu.SemaphoreType.DMA((8,)),
         ],
-        compiler_params=pltpu.CompilerParams(collective_id=0, has_side_effects=True),
+        compiler_params=pltpu.CompilerParams(collective_id=0, has_side_effects=True, vmem_limit_bytes=60 << 20),
         name="spread",
     )(tokens, out_grad, ids, w_cat)
 
@@ -161,83 +296,140 @@
     return grad_gate.astype(BF16), grad_up.astype(BF16), hidden.astype(BF16)
 
 
-MIDDLE_COPIES = 8 + 4 + 1 + 3 + 2 + 4
-
-
-def middle_kernel(part, weight, h_out, ra, rb, sa, sb, fl, fr, zs, zr, own, send_sem, recv_sem, own_sem):
+MIDDLE_COPIES = 13 + 10 + 9 + 8
+
+
+def middle_kernel(
+    part, weight, h_out, ra, rb, sa, sb, fl, fr, zs, zr, zin, s2, s1, s3, ra2, rb2, sa2, sb2, fl2, fr2, own,
+    send_sem, recv_sem, own_sem,
+):
     me = Spot()
     right, left, pair = me.to(y=1), me.to(y=3), me.to(zl=1)
     greet([right, left, pair])
     links = Links(send_sem, recv_sem)
-    low, high = pl.ds(0, 128), pl.ds(128, 128)
-
-    first_a, first_b, other_b, other_a, last_a, last_b = {}, {}, {}, {}, {}, {}
+    low, high = pl.ds(0, 64), pl.ds(64, 64)
+    k0, k1, k1_low, k1_high = pl.ds(0, 128), pl.ds(128, 128), pl.ds(128, 64), pl.ds(192, 64)
+
+    first_a, first_b, other_b, other_a, last_a, last_b, z_in = {}, {}, {}, {}, {}, {}, {}
+    z_in[2] = links.send(part.at[me.block(2, 1), k1, :], zin.at[2], pair)
     for dz in (1, 0):
         first_a[dz] = links.send(part.at[me.block(2, dz), low, :], ra.at[dz], right)
         first_b[dz] = links.send(part.at[me.block(2, dz), high, :], rb.at[dz], left)
+    for y in (1, 3, 0):
+        z_in[y] = links.send(part.at[me.block(y, 1), k1, :], zin.at[y], pair)
     for dz in (1, 0):
         other_b[dz] = links.send(part.at[me.block(1, dz), high, :], fl.at[dz, high, :], right)
         other_a[dz] = links.send(part.at[me.block(3, dz), low, :], fr.at[dz, low, :], left)
-    for dz in (1, 0):
+
+    def relay(dz):
         first_a[dz].wait_recv()
-        add_rows(sa.at[dz], [part.at[me.block(1, dz), low, :], ra.at[dz]], 128)
+        add_rows(sa.at[dz], [part.at[me.block(1, dz), low, :], ra.at[dz]], 64)
         last_a[dz] = links.send(sa.at[dz], fl.at[dz, low, :], right)
         first_b[dz].wait_recv()
-        add_rows(sb.at[dz], [part.at[me.block(3, dz), high, :], rb.at[dz]], 128)
+        add_rows(sb.at[dz], [part.at[me.block(3, dz), high, :], rb.at[dz]], 64)
         last_b[dz] = links.send(sb.at[dz], fr.at[dz, high, :], left)
+
+    relay(1)
+    z_in[2].wait_recv()
+    add_rows(s2, [part.at[me.block(2, 0), k1, :], zin.at[2]], 128)
+    far_a = links.send(s2.at[low, :], ra2, right)
+    far_b = links.send(s2.at[high, :], rb2, left)
+    relay(0)
+    z_in[1].wait_recv()
+    add_rows(s1, [part.at[me.block(1, 0), k1_high, :], zin.at[1, high, :]], 64)
+    side_b = links.send(s1, fl2.at[high, :], right)
     for group in (other_b, other_a, last_a, last_b):
         group[1].wait_recv()
-    add_rows(zs, [part.at[me.block(0, 1)], fl.at[1], fr.at[1]], 256)
+    add_rows(zs, [part.at[me.block(0, 1), k0, :], fl.at[1], fr.at[1]], 128)
     cross = links.send(zs, zr, pair)
+    z_in[3].wait_recv()
+    add_rows(s3, [part.at[me.block(3, 0), k1_low, :], zin.at[3, low, :]], 64)
+    side_a = links.send(s3, fr2.at[low, :], left)
+    far_a.wait_recv()
+    add_rows(sa2, [part.at[me.block(1, 0), k1_low, :], zin.at[1, low, :], ra2], 64)
+    end_a = links.send(sa2, fl2.at[low, :], right)
+    far_b.wait_recv()
+    add_rows(sb2, [part.at[me.block(3, 0), k1_high, :], zin.at[3, high, :], rb2], 64)
+    end_b = links.send(sb2, fr2.at[high, :], left)
+
+    def active(start, sources):
+        @pl.loop(0, 8)
+        def _(i):
+            row = pl.multiple_of(i * 16, 16)
+            at = pl.ds(start + row, 16)
+            pre = part[me.b, at, :].astype(F32)
+            for source in sources:
+                pre = pre + source[pl.ds(row, 16), :].astype(F32)
+            own[at, :256], own[at, 256:512], own[at, 512:] = activation(pre, weight[at, :])
+
     for group in (other_b, other_a, last_a, last_b):
         group[0].wait_recv()
     cross.wait_recv()
-
-    @pl.loop(0, 16)
-    def _(i):
-        at = pl.ds(pl.multiple_of(i * 16, 16), 16)
-        pre = part[me.block(0, 0), at, :].astype(F32) + zr[at, :].astype(F32)
-        pre = pre + fl[0, at, :].astype(F32) + fr[0, at, :].astype(F32)
-        own[at, :256], own[at, 256:512], own[at, 512:] = activation(pre, weight[at, :])
-
-    mine = pltpu.make_async_copy(own, h_out.at[me.q], own_sem)
-    mine.start()
-    from_pair = links.send(own, h_out.at[me.q], pair)
-    from_left0 = links.send(own, h_out.at[me.q], right)
-    from_right0 = links.send(own, h_out.at[me.q], left)
-
-    def pass_on(block, device, rows=pl.ds(0, 256)):
+    active(0, [fl.at[0], fr.at[0], zr])
+    mine0 = pltpu.make_async_copy(own.at[k0, :], h_out.at[me.b, k0, :], own_sem.at[0])
+    mine0.start()
+    from_pair = links.send(own.at[k0, :], h_out.at[me.b, k0, :], pair)
+    from_left = {0: links.send(own.at[k0, :], h_out.at[me.b, k0, :], right)}
+    from_right = {0: links.send(own.at[k0, :], h_out.at[me.b, k0, :], left)}
+
+    def pass_on(block, device, rows):
         piece = h_out.at[block, rows, :]
         return links.send(piece, piece, device)
 
+    for copy in (z_in[0], side_a, side_b, end_a, end_b):
+        copy.wait_recv()
+    active(128, [zin.at[0], fl2, fr2])
+    mine1 = pltpu.make_async_copy(own.at[k1, :], h_out.at[me.b, k1, :], own_sem.at[1])
+    mine1.start()
+    left1 = links.send(own.at[k1, :], h_out.at[me.b, k1, :], right)
+    right1 = links.send(own.at[k1, :], h_out.at[me.b, k1, :], left)
+    tail = [links.send(own.at[k1, :], h_out.at[me.b, k1, :], pair)]
     from_pair.wait_recv()
-    from_left1 = pass_on(me.block(0, 1), right)
-    from_right1 = pass_on(me.block(0, 1), left)
-    halves = []
-    for dz, from_left, from_right in ((0, from_left0, from_right0), (1, from_left1, from_right1)):
-        from_left.wait_recv()
-        halves.append(pass_on(me.block(3, dz), right, low))
-        from_right.wait_recv()
-        halves.append(pass_on(me.block(1, dz), left, high))
-    for half in halves:
-        half.wait_recv()
-    mine.wait()
+    from_left[1] = pass_on(me.block(0, 1), right, k0)
+    from_right[1] = pass_on(me.block(0, 1), left, k0)
+    from_left[0].wait_recv()
+    tail.append(pass_on(me.block(3, 0), right, low))
+    from_right[0].wait_recv()
+    tail.append(pass_on(me.block(1, 0), left, high))
+    left1.wait_recv()
+    half_a = pass_on(me.block(3, 0), right, k1_low)
+    tail.append(pass_on(me.block(3, 0), pair, k1))
+    right1.wait_recv()
+    half_b = pass_on(me.block(1, 0), left, k1_high)
+    tail.append(pass_on(me.block(1, 0), pair, k1))
+    from_left[1].wait_recv()
+    tail.append(pass_on(me.block(3, 1), right, low))
+    from_right[1].wait_recv()
+    tail.append(pass_on(me.block(1, 1), left, high))
+    half_a.wait_recv()
+    half_b.wait_recv()
+    tail.append(pass_on(me.block(2, 0), pair, k1))
+    for copy in tail:
+        copy.wait_recv()
+    mine0.wait()
+    mine1.wait()
     links.finish()
 
 
 def middle(part, weight):
     vmem, anywhere = pl.BlockSpec(memory_space=pltpu.VMEM), pl.BlockSpec(memory_space=pl.ANY)
-    half, full = pltpu.VMEM((2, 128, 768), BF16), pltpu.VMEM((2, 256, 768), BF16)
-    one = pltpu.VMEM((256, 768), BF16)
+    rows = lambda *shape: pltpu.VMEM(shape + (768,), BF16)
     return pl.pallas_call(
         middle_kernel,
         out_shape=jax.ShapeDtypeStruct((8, 256, 768), BF16),
         in_specs=[vmem] * 2,
         out_specs=anywhere,
-        scratch_shapes=[half] * 4 + [full] * 2 + [one] * 3 + [
+        scratch_shapes=[rows(2, 64)] * 4
+        + [rows(2, 128)] * 2
+        + [rows(128)] * 2
+        + [rows(4, 128), rows(128)]
+        + [rows(64)] * 6
+        + [rows(128)] * 2
+        + [
+            rows(256),
             pltpu.SemaphoreType.DMA((MIDDLE_COPIES,)),
             pltpu.SemaphoreType.DMA((MIDDLE_COPIES,)),
-            pltpu.SemaphoreType.DMA,
+            pltpu.SemaphoreType.DMA((2,)),
         ],
         compiler_params=pltpu.CompilerParams(collective_id=1, has_side_effects=True),
         name="middle",
@@ -249,8 +441,8 @@
 
 
 def finish_kernel(
-    x, og, ids, h, w, d_out, g_out,
-    xt, ogt, w_all, he, g, cr, dx, a2, ra, rb, sa, sb, oa, ob, fl, fr, zs, zr,
+    xt, ogt, ids, h, w, d_out, g_out,
+    w_all, he, g, cr, dx, a2, ra, rb, sa, sb, oa, ob, fl, fr, zs, zr,
     send_sem, recv_sem, w_sem, own_sem,
 ):
     me = Spot()
@@ -258,9 +450,6 @@
     loads = [pltpu.make_async_copy(w.at[e], w_all.at[e], w_sem.at[e]) for e in range(8)]
     for load in loads:
         load.start()
-    for q in range(8):
-        xt[:, q * 128 : q * 128 + 128] = jnp.transpose(x[q])
-        ogt[:, q * 128 : q * 128 + 128] = jnp.transpose(og[q])
     greet([me.to(y=dy, zl=dz) for dy, dz in PEERS] + [right, left, core, far])
     links = Links(send_sem, recv_sem)
     low, high = pl.ds(0, 192), pl.ds(192, 192)
@@ -344,10 +533,10 @@
     token_part(1)
     token_part(2)
     back = []
-    cols = pl.ds(pl.multiple_of(me.q * 768, 768), 768)
+    cols = me.columns(0, 0)
     for dy, dz in PEERS:
         back.append(links.send(dx.at[me.block(dy, dz)], d_out.at[:, cols], me.to(y=dy, zl=dz)))
-    keep = pltpu.make_async_copy(dx.at[me.q], d_out.at[:, cols], own_sem)
+    keep = pltpu.make_async_copy(dx.at[me.b], d_out.at[:, cols], own_sem)
     keep.start()
     relay(0)
     for group in (other_b, other_a, last_a, last_b):
@@ -368,7 +557,7 @@
     links.finish()
 
 
-def finish(x, og, ids, h, w):
+def finish(xt, ogt, ids, h, w):
     vmem, anywhere = pl.BlockSpec(memory_space=pltpu.VMEM), pl.BlockSpec(memory_space=pl.ANY)
     half, full = pltpu.VMEM((2, 192, 768), BF16), pltpu.VMEM((2, 384, 768), BF16)
     one = pltpu.VMEM((384, 768), BF16)
@@ -381,8 +570,6 @@
         in_specs=[vmem] * 4 + [anywhere],
         out_specs=(anywhere, vmem),
         scratch_shapes=[
-            pltpu.VMEM((768, 1024), BF16),
-            pltpu.VMEM((768, 1024), BF16),
             pltpu.VMEM((8, 768, 768), BF16),
             pltpu.VMEM((8, 1024, 768), BF16),
             pltpu.VMEM((8, 2, 384, 768), BF16),
@@ -398,34 +585,15 @@
         ],
         compiler_params=pltpu.CompilerParams(collective_id=2, has_side_effects=True, vmem_limit_bytes=60 << 20),
         name="finish",
-    )(x, og, ids, h, w)
-
-
-def partial_pre(x, og, ids_all, w):
-    total = [jnp.zeros((1024, 768), F32) for _ in range(2)]
-    for e in range(8):
-        y = jnp.concatenate(
-            [
-                jnp.dot(x, w[e, :, :512], preferred_element_type=F32),
-                jnp.dot(og, w[e, :, 512:], preferred_element_type=F32),
-            ],
-            axis=1,
-        )
-        for k in range(2):
-            total[k] = jnp.where(ids_all[:, k : k + 1] == e, y, total[k])
-    both = jnp.stack([t.reshape(8, 128, 768) for t in total], axis=1)
-    return both.reshape(8, 256, 768).astype(BF16)
+    )(xt, ogt, ids, h, w)
 
 
 def shards(tokens, out_grad, expert_ids, route_weight, w_gate, w_up, w_down):
     w_cat = jnp.concatenate([w_gate[0], w_up[0], jnp.transpose(w_down[0])], axis=1)
     ids = jnp.zeros((8, 128), jnp.int32).at[:2].set(jnp.transpose(expert_ids))
-    x, og, ids_all, w = spread(tokens, out_grad, ids, w_cat)
-    w = w.reshape(8, 768, 768)
-    ids_all = jnp.transpose(ids_all[:, :2], (0, 2, 1)).reshape(1024, 2)
-    part = partial_pre(x.reshape(1024, 768), og.reshape(1024, 768), ids_all, w)
+    part, xt, ogt, names, w = spread(tokens, out_grad, ids, w_cat)
     h = middle(part, jnp.transpose(route_weight).reshape(256, 1))
-    d_tokens, g = finish(x, og, ids_all, h, w)
+    d_tokens, g = finish(xt, ogt, names, h, w.reshape(8, 768, 768))
     return d_tokens, g[None, :, :256], g[None, :, 256:512], jnp.transpose(g[:, 512:])[None]
 
 

time: 286 us -> 226 us (0.79)
  matrix products: 29.6 us -> 0 us
  Pallas kernels: 230 us -> 215 us
  other arithmetic: 15.9 us -> 1.88 us
    dot_general x16 -> x0, matrix products: 29.6 us -> none  [the longest x8 17.2 us: partial_pre(): jnp.dot(x, w[e, :, :512], preferred_element_type=F32)]
    pallas_call x1, Pallas kernels: 61.8 us -> 48.5 us  [middle(): pl.pallas_call(middle_kernel, out_shape=jax.ShapeDtypeStruct((8, 256, 768...]
    another operation x3 -> x0, other arithmetic: 11.5 us -> none
where the time goes in v1:
time: 226 us
  Pallas kernels  215 us (95%)
  local copies, waits for them, and re-layouts  8.18 us (4%)
    pallas_call x1, Pallas kernels, finish(): pl.pallas_call(finish_kernel, out_shape=(jax.ShapeDtypeStruct((128, 6144)...  85.8 us
    pallas_call x1, Pallas kernels, spread(): pl.pallas_call(spread_kernel, out_shape=(jax.ShapeDtypeStruct((8, 256, 76...  80.9 us
    pallas_call x1, Pallas kernels, middle(): pl.pallas_call(middle_kernel, out_shape=jax.ShapeDtypeStruct((8, 256, 768...  48.5 us

profile of v1, /device:TPU:1, one launch (start us, length us, event | category | flops | bytes accessed | tf_op | source)
XLA Modules:
  0.0 225.9 jit_solution(4732456774267034834)
XLA Ops:
  0.6 1.3 scatter.4.ids
  1.9 1.5 copy.14.weight
  3.4 1.1 copy.13
  4.4 1.9 pad_maximum_fusion.w_in
  6.3 80.9 %spread.1 = (bf16[8,256,768]{2,1,0:T(8,128)(2,1)}, bf16[768,1024]{1,0:T(8,128)(2,1)}, bf16[768,1024]{1,0:T(8,128)(2,1)}, s32[1024,8]{1,0:T(8,128)}, bf16[8,2,384,768]{3,2,1,0:T(8,128)(2,1)}) custom-call(bf16[128,6144]{1,0:T(8,128)(2,1)} %tok.1, bf16[128,6144]{1,0:T(8,128)(2,1)} %og.1, s32[8,128]{1,0:T(8,128)} %scatter.4.ids, ...), custom_call_target="tpu_custom_call" | custom-call | tf_op jit(solution)/shard_map/spread/pallas_call | solution.py:259
  87.2 48.5 %middle.1.h = bf16[8,256,768]{2,1,0:T(8,128)(2,1)} custom-call(bf16[8,256,768]{2,1,0:T(8,128)(2,1)} %get-tuple-element.26.part, f32[256,1]{1,0:T(8,128)} %copy.14.weight), custom_call_target="tpu_custom_call" | custom-call | tf_op jit(solution)/shard_map/middle/pallas_call | solution.py:417
  135.7 85.8 %finish.1 = (bf16[128,6144]{1,0:T(8,128)(2,1)}, f32[384,768]{1,0:T(8,128)}) custom-call(bf16[768,1024]{1,0:T(8,128)(2,1)} %get-tuple-element.23.xt, bf16[768,1024]{1,0:T(8,128)(2,1)} %get-tuple-element.24.ogt, s32[1024,8]{1,0:T(8,128)} %get-tuple-element.25.ids, bf16[8,256,768]{2,1,0:T(8,128)(2,1)} %middle.1.h, bf16[8,768,768]{2,1,0:T(8,128)(2,1)} %bitcast.18), custom_call_target="tpu_custom_call" | custom-call | tf_op jit(solution)/shard_map/finish/pallas_call | solution.py:564
  221.6 0.0 copy-start
  221.6 2.3 %slice_bitcast_fusion = (f32[1,256,384]{1,2,0:T(8,128)S(1)}, f32[1,384,256]{2,1,0:T(8,128)}, f32[1,384,256]{2,1,0:T(8,128)}) fusion(f32[384,768]{1,0:T(8,128)} %get-tuple-element.29), kind=kLoop, calls=%fused_computation.1 | loop fusion | bytes 2359296 | tf_op jit(solution)/shard_map/broadcast_in_dim | solution.py:597
  223.9 0.9 copy.15
  224.8 0.0 copy-done
  224.8 1.1 copy.17
Async XLA Ops:
  221.6 3.2 %copy-start = (bf16[128,6144]{1,0:T(8,128)(2,1)S(1)}, bf16[128,6144]{1,0:T(8,128)(2,1)}, u32[]{:S(2)}) copy-start(bf16[128,6144]{1,0:T(8,128)(2,1)} %get-tuple-element.45) | copy-start | bytes 4718596

commit v2 on v1

--- a/solution.py
+++ b/solution.py
@@ -80,12 +80,17 @@
 
 
 def spread_kernel(
-    tok, og, ids, w_in, part, xt, ogt, idc, w_out,
-    x, g, ids_in, w, z_tok, z_og, l_tok, r_og, send_sem, recv_sem, own_sem, w_sem,
+    tok, og, ids_rows, gate_in, up_in, down_in, part, xt, ogt, idc, w_out,
+    w_in, ids, x, g, ids_in, w, z_tok, z_og, l_tok, r_og, send_sem, recv_sem, own_sem, w_sem,
 ):
     me = Spot()
     right, left, up, down = me.to(x=1), me.to(x=3), me.to(y=1), me.to(y=3)
     core, far, pair = me.to(c=1), me.to(zh=1), me.to(zl=1)
+    w_in[:, :256] = gate_in[...]
+    w_in[:, 256:512] = up_in[...]
+    w_in[:, 512:] = jnp.transpose(down_in[...])
+    ids[...] = jnp.zeros((8, 128), jnp.int32)
+    ids[:2, :] = ids_rows[...]
     greet([me.to(y=dy, zl=dz) for dy, dz in PEERS] + [right, left, core, far])
     links = Links(send_sem, recv_sem)
     own, far_e = me.expert(0, 0), me.expert(0, 1)
@@ -253,7 +258,7 @@
         pltpu.make_async_copy(w.at[e], w_out.at[e], w_sem.at[e]).wait()
 
 
-def spread(tokens, out_grad, ids, w_cat):
+def spread(tokens, out_grad, ids, w_gate, w_up, w_down):
     vmem, anywhere = pl.BlockSpec(memory_space=pltpu.VMEM), pl.BlockSpec(memory_space=pl.ANY)
     blocks = lambda n: pltpu.VMEM((n, 128, 768), BF16)
     return pl.pallas_call(
@@ -265,9 +270,11 @@
             jax.ShapeDtypeStruct((1024, 8), jnp.int32),
             jax.ShapeDtypeStruct((8, 2, 384, 768), BF16),
         ),
-        in_specs=[vmem] * 4,
+        in_specs=[vmem] * 6,
         out_specs=(vmem,) * 4 + (anywhere,),
         scratch_shapes=[
+            pltpu.VMEM((384, 768), BF16),
+            pltpu.VMEM((8, 128), jnp.int32),
             blocks(8),
             blocks(8),
             pltpu.VMEM((8, 8, 128), jnp.int32),
@@ -283,7 +290,7 @@
         ],
         compiler_params=pltpu.CompilerParams(collective_id=0, has_side_effects=True, vmem_limit_bytes=60 << 20),
         name="spread",
-    )(tokens, out_grad, ids, w_cat)
+    )(tokens, out_grad, ids, w_gate, w_up, w_down)
 
 
 def activation(pre, weight):
@@ -300,11 +307,14 @@
 
 
 def middle_kernel(
-    part, weight, h_out, ra, rb, sa, sb, fl, fr, zs, zr, zin, s2, s1, s3, ra2, rb2, sa2, sb2, fl2, fr2, own,
+    part, weight_rows, h_out, weight8, weight, ra, rb, sa, sb, fl, fr, zs, zr, zin, s2, s1, s3, ra2, rb2, sa2, sb2, fl2, fr2, own,
     send_sem, recv_sem, own_sem,
 ):
     me = Spot()
     right, left, pair = me.to(y=1), me.to(y=3), me.to(zl=1)
+    weight8[...] = jnp.zeros((8, 128), F32)
+    weight8[:2, :] = weight_rows[...]
+    weight[...] = jnp.transpose(weight8[...])
     greet([right, left, pair])
     links = Links(send_sem, recv_sem)
     low, high = pl.ds(0, 64), pl.ds(64, 64)
@@ -352,15 +362,15 @@
     add_rows(sb2, [part.at[me.block(3, 0), k1_high, :], zin.at[3, high, :], rb2], 64)
     end_b = links.send(sb2, fr2.at[high, :], left)
 
-    def active(start, sources):
+    def active(k, sources):
         @pl.loop(0, 8)
         def _(i):
             row = pl.multiple_of(i * 16, 16)
-            at = pl.ds(start + row, 16)
+            at = pl.ds(k * 128 + row, 16)
             pre = part[me.b, at, :].astype(F32)
             for source in sources:
                 pre = pre + source[pl.ds(row, 16), :].astype(F32)
-            own[at, :256], own[at, 256:512], own[at, 512:] = activation(pre, weight[at, :])
+            own[at, :256], own[at, 256:512], own[at, 512:] = activation(pre, weight[pl.ds(row, 16), k : k + 1])
 
     for group in (other_b, other_a, last_a, last_b):
         group[0].wait_recv()
@@ -378,7 +388,7 @@
 
     for copy in (z_in[0], side_a, side_b, end_a, end_b):
         copy.wait_recv()
-    active(128, [zin.at[0], fl2, fr2])
+    active(1, [zin.at[0], fl2, fr2])
     mine1 = pltpu.make_async_copy(own.at[k1, :], h_out.at[me.b, k1, :], own_sem.at[1])
     mine1.start()
     left1 = links.send(own.at[k1, :], h_out.at[me.b, k1, :], right)
@@ -419,7 +429,8 @@
         out_shape=jax.ShapeDtypeStruct((8, 256, 768), BF16),
         in_specs=[vmem] * 2,
         out_specs=anywhere,
-        scratch_shapes=[rows(2, 64)] * 4
+        scratch_shapes=[pltpu.VMEM((8, 128), F32), pltpu.VMEM((128, 8), F32)]
+        + [rows(2, 64)] * 4
         + [rows(2, 128)] * 2
         + [rows(128)] * 2
         + [rows(4, 128), rows(128)]
@@ -441,8 +452,8 @@
 
 
 def finish_kernel(
-    xt, ogt, ids, h, w, d_out, g_out,
-    w_all, he, g, cr, dx, a2, ra, rb, sa, sb, oa, ob, fl, fr, zs, zr,
+    xt, ogt, ids, h, w, d_out, gate_out, up_out, down_out,
+    w_all, he, g, cr, dx, g_out, a2, ra, rb, sa, sb, oa, ob, fl, fr, zs, zr,
     send_sem, recv_sem, w_sem, own_sem,
 ):
     me = Spot()
@@ -459,15 +470,14 @@
     def product(step, dz):
         e = me.expert(step, dz)
 
-        @pl.loop(0, 32)
-        def _(i):
-            at = pl.ds(pl.multiple_of(i * 32, 32), 32)
-            q, row = i // 4, pl.multiple_of(i % 4 * 32, 32)
-            m0 = (ids[at, 0:1] == e).astype(F32)
-            m1 = (ids[at, 1:2] == e).astype(F32)
-            h0 = h[q, pl.ds(row, 32), :].astype(F32)
-            h1 = h[q, pl.ds(row + 128, 32), :].astype(F32)
-            he[e, at, :] = (h0 * m0 + h1 * m1).astype(BF16)
+        @pl.loop(0, 8)
+        def _(q):
+            at = pl.ds(pl.multiple_of(q * 128, 128), 128)
+            chosen = [(ids[at, k : k + 1] == e).astype(F32) for k in range(2)]
+            m0, m1 = [jnp.broadcast_to(m, (128, 128)).astype(BF16) for m in chosen]
+            for n in range(6):
+                cols = slice(n * 128, n * 128 + 128)
+                he[e, at, cols] = h[q, :128, cols] * m0 + h[q, 128:, cols] * m1
 
         for n, left_t in ((0, xt), (1, xt), (2, ogt)):
             cols = slice(n * 256, n * 256 + 256)
@@ -551,6 +561,9 @@
     cross.wait_recv()
     e = me.expert(0, 0)
     add_rows(g_out, [g.at[e, mine], cr.at[e], fl.at[0], fr.at[0], zr], 384)
+    gate_out[...] = g_out[:, :256]
+    up_out[...] = g_out[:, 256:512]
+    down_out[...] = jnp.transpose(g_out[:, 512:])
     for copy in back:
         copy.wait_recv()
     keep.wait()
@@ -565,16 +578,19 @@
         finish_kernel,
         out_shape=(
             jax.ShapeDtypeStruct((128, 6144), BF16),
-            jax.ShapeDtypeStruct((384, 768), F32),
+            jax.ShapeDtypeStruct((384, 256), F32),
+            jax.ShapeDtypeStruct((384, 256), F32),
+            jax.ShapeDtypeStruct((256, 384), F32),
         ),
         in_specs=[vmem] * 4 + [anywhere],
-        out_specs=(anywhere, vmem),
+        out_specs=(anywhere,) + (vmem,) * 3,
         scratch_shapes=[
             pltpu.VMEM((8, 768, 768), BF16),
             pltpu.VMEM((8, 1024, 768), BF16),
             pltpu.VMEM((8, 2, 384, 768), BF16),
             pltpu.VMEM((8, 384, 768), BF16),
             pltpu.VMEM((8, 128, 768), BF16),
+            pltpu.VMEM((384, 768), F32),
         ]
         + [full] + [half] * 6 + [full] * 2 + [one] * 2
         + [
@@ -589,12 +605,10 @@
 
 
 def shards(tokens, out_grad, expert_ids, route_weight, w_gate, w_up, w_down):
-    w_cat = jnp.concatenate([w_gate[0], w_up[0], jnp.transpose(w_down[0])], axis=1)
-    ids = jnp.zeros((8, 128), jnp.int32).at[:2].set(jnp.transpose(expert_ids))
-    part, xt, ogt, names, w = spread(tokens, out_grad, ids, w_cat)
-    h = middle(part, jnp.transpose(route_weight).reshape(256, 1))
-    d_tokens, g = finish(xt, ogt, names, h, w.reshape(8, 768, 768))
-    return d_tokens, g[None, :, :256], g[None, :, 256:512], jnp.transpose(g[:, 512:])[None]
+    part, xt, ogt, names, w = spread(tokens, out_grad, jnp.transpose(expert_ids), w_gate[0], w_up[0], w_down[0])
+    h = middle(part, jnp.transpose(route_weight))
+    d_tokens, gate, up, down = finish(xt, ogt, names, h, w.reshape(8, 768, 768))
+    return d_tokens, gate[None], up[None], down[None]
 
 
 def solution(mesh):

time: 226 us -> 208 us (0.920)
  Pallas kernels: 215 us -> 202 us
  local copies, waits for them, and re-layouts: 8.18 us -> 5.01 us
    pallas_call x1, Pallas kernels: 85.8 us -> 72.6 us  [finish(): pl.pallas_call(finish_kernel, out_shape=(jax.ShapeDtypeStruct((128, 6144)...]
    broadcast_in_dim x1 -> x0, local copies, waits for them, and re-layouts: 2.31 us -> none  [shards(): jnp.transpose(g[:, 512:])[None]]
    unnamed x5 -> x10, local copies, waits for them, and re-layouts: 3.12 us -> 5.01 us
where the time goes in v2:
time: 208 us
  Pallas kernels  202 us (97%)
  local copies, waits for them, and re-layouts  5.01 us (2%)
    pallas_call x1, Pallas kernels, spread(): pl.pallas_call(spread_kernel, out_shape=(jax.ShapeDtypeStruct((8, 256, 76...  81 us
    pallas_call x1, Pallas kernels, finish(): pl.pallas_call(finish_kernel, out_shape=(jax.ShapeDtypeStruct((128, 6144)...  72.6 us
    pallas_call x1, Pallas kernels, middle(): pl.pallas_call(middle_kernel, out_shape=jax.ShapeDtypeStruct((8, 256, 768...  48.9 us
    unnamed x10, local copies, waits for them, and re-layouts  5.01 us

profile of v2, /device:TPU:1, one launch (start us, length us, event | category | flops | bytes accessed | tf_op | source)
XLA Modules:
  0.0 208.1 jit_solution(601195470087642095)
XLA Ops:
  0.6 81.0 %spread.1 = (bf16[8,256,768]{2,1,0:T(8,128)(2,1)}, bf16[768,1024]{1,0:T(8,128)(2,1)}, bf16[768,1024]{1,0:T(8,128)(2,1)}, s32[1024,8]{1,0:T(8,128)}, bf16[8,2,384,768]{3,2,1,0:T(8,128)(2,1)}) custom-call(bf16[128,6144]{1,0:T(8,128)(2,1)} %tok.1, bf16[128,6144]{1,0:T(8,128)(2,1)} %og.1, s32[2,128]{1,0:T(2,128)} %bitcast.16, bf16[384,256]{1,0:T(8,128)(2,1)} %bitcast.13, ...), custom_call_target="tpu_custom_call" | custom-call | tf_op jit(solution)/shard_map/spread/pallas_call | solution.py:264
  81.6 48.9 %middle.1.h = bf16[8,256,768]{2,1,0:T(8,128)(2,1)} custom-call(bf16[8,256,768]{2,1,0:T(8,128)(2,1)} %get-tuple-element.16.part, f32[2,128]{1,0:T(2,128)} %bitcast.17), custom_call_target="tpu_custom_call" | custom-call | tf_op jit(solution)/shard_map/middle/pallas_call | solution.py:427
  130.5 72.6 %finish.1 = (bf16[128,6144]{1,0:T(8,128)(2,1)}, f32[384,256]{1,0:T(8,128)}, f32[384,256]{1,0:T(8,128)}, f32[256,384]{1,0:T(8,128)}) custom-call(bf16[768,1024]{1,0:T(8,128)(2,1)} %get-tuple-element.13.xt, bf16[768,1024]{1,0:T(8,128)(2,1)} %get-tuple-element.14.ogt, s32[1024,8]{1,0:T(8,128)} %get-tuple-element.15.ids, bf16[8,256,768]{2,1,0:T(8,128)(2,1)} %middle.1.h, ...), custom_call_target="tpu_custom_call" | custom-call | tf_op jit(solution)/shard_map/finish/pallas_call | solution.py:577
  203.1 0.0 copy-start.2
  203.1 0.0 copy-start.1
  203.1 2.8 %copy.15 = bf16[128,6144]{1,0:T(8,128)(2,1)} copy(bf16[128,6144]{1,0:T(8,128)(2,1)} %get-tuple-element.26) | data formatting | bytes 3145728
  205.9 0.0 copy-done.2
  205.9 0.0 copy-start
  205.9 0.7 copy.16
  206.6 0.0 copy-done.1
  206.6 0.7 copy.17
  207.4 0.0 copy-done
  207.4 0.7 copy.18
Async XLA Ops:
  203.1 2.8 %copy-start.2 = (f32[384,256]{1,0:T(8,128)S(1)}, f32[384,256]{1,0:T(8,128)}, u32[]{:S(2)}) copy-start(f32[384,256]{1,0:T(8,128)} %get-tuple-element.19) | copy-start | bytes 1179652
  203.1 3.5 %copy-start.1 = (f32[384,256]{1,0:T(8,128)S(1)}, f32[384,256]{1,0:T(8,128)}, u32[]{:S(2)}) copy-start(f32[384,256]{1,0:T(8,128)} %get-tuple-element.20) | copy-start | bytes 1179652
  205.9 1.5 copy-start

commit v3 on v2

v3 whole, which is shorter than its diff:
```python
import functools

import jax
import jax.numpy as jnp
from jax import lax
from jax.experimental import pallas as pl
from jax.experimental.pallas import tpu as pltpu
from jax.sharding import PartitionSpec as P

MESH = pl.DeviceIdType.MESH
F32, BF16 = jnp.float32, jnp.bfloat16
PEERS = [(dy, dz) for dy in (2, 1, 3, 0) for dz in (1, 0) if (dy, dz) != (0, 0)]


class Spot:
    def __init__(self):
        dp, ep = lax.axis_index("dp"), lax.axis_index("ep")
        self.y, self.zl, self.c = dp // 4, (dp // 2) % 2, dp % 2
        self.zh, self.x = ep // 4, ep % 4
        self.b = self.block(0, 0)

    def to(self, y=0, zl=0, c=0, zh=0, x=0):
        dp = (self.y + y) % 4 * 4 + (self.zl + zl) % 2 * 2 + (self.c + c) % 2
        return (dp, (self.zh + zh) % 2 * 4 + (self.x + x) % 4)

    def block(self, y, zl):
        return (self.zl + zl) % 2 * 4 + (self.y + y) % 4

    def columns(self, y, zl, width=768, offset=0):
        start = ((self.y + y) % 4 * 2 + (self.zl + zl) % 2) * 768 + offset
        return pl.ds(pl.multiple_of(start, 128), width)

    def expert(self, x, zh):
        return (self.zh + zh) % 2 * 4 + (self.x + x) % 4


class Links:
    def __init__(self, send_sem, recv_sem):
        self.send_sem, self.recv_sem, self.count, self.sent = send_sem, recv_sem, 0, []

    def send(self, src, dst, device):
        n = self.count
        self.count += 1
        copy = pltpu.make_async_remote_copy(
            src_ref=src,
            dst_ref=dst,
            send_sem=self.send_sem.at[n],
            recv_sem=self.recv_sem.at[n],
            device_id=device,
            device_id_type=MESH,
        )
        copy.start()
        self.sent.append(copy)
        return copy

    def finish(self):
        assert self.count == self.send_sem.shape[0]
        for copy in self.sent:
            copy.wait_send()


def greet(devices):
    barrier = pltpu.get_barrier_semaphore()
    for device in devices:
        pl.semaphore_signal(barrier, inc=1, device_id=device, device_id_type=MESH)
    pl.semaphore_wait(barrier, len(devices))


def add_rows(dst, sources, rows, step=32):
    @pl.loop(0, rows // step)
    def _(i):
        at = pl.ds(pl.multiple_of(i * step, step), step)
        total = sources[0][at, :].astype(F32)
        for source in sources[1:]:
            total = total + source[at, :].astype(F32)
        dst[at, :] = total.astype(dst.dtype)


def activation(pre, weight):
    gate, up, grad_hidden = pre[:, :256], pre[:, 256:512], pre[:, 512:] * weight
    sig = jax.nn.sigmoid(gate)
    silu = gate * sig
    hidden = silu * up * weight
    grad_gate = grad_hidden * up * sig * (1.0 + gate * (1.0 - sig))
    grad_up = grad_hidden * silu
    return grad_gate.astype(BF16), grad_up.astype(BF16), hidden.astype(BF16)


def open_sums(me, links, part, dz, sums):
    ra, rb, fl, fr = sums[2], sums[3], sums[6], sums[7]
    right, left = me.to(y=1), me.to(y=3)
    low, high = pl.ds(0, 64), pl.ds(64, 64)
    return (
        links.send(part.at[me.block(2, dz), low, :], ra.at[dz], right),
        links.send(part.at[me.block(2, dz), high, :], rb.at[dz], left),
        links.send(part.at[me.block(1, dz), high, :], fl.at[dz, high, :], right),
        links.send(part.at[me.block(3, dz), low, :], fr.at[dz, low, :], left),
    )


def close_sums(me, links, part, weight_rows, h_out, opened, sums):
    (
        weight8, weight, ra, rb, sa, sb, fl, fr, zs, zr, zin, s2, s1, s3, ra2, rb2, sa2, sb2, fl2, fr2, own, h_sem,
    ) = sums
    right, left, pair = me.to(y=1), me.to(y=3), me.to(zl=1)
    low, high = pl.ds(0, 64), pl.ds(64, 64)
    k0, k1, k1_low, k1_high = pl.ds(0, 128), pl.ds(128, 128), pl.ds(128, 64), pl.ds(192, 64)
    z_in = {2: links.send(part.at[me.block(2, 1), k1, :], zin.at[2], pair)}
    opened[1] = open_sums(me, links, part, 1, sums)
    first_a, first_b, other_b, other_a = [{dz: opened[dz][n] for dz in (0, 1)} for n in range(4)]
    last_a, last_b = {}, {}
    for y in (1, 3, 0):
        z_in[y] = links.send(part.at[me.block(y, 1), k1, :], zin.at[y], pair)
    weight8[...] = jnp.zeros((8, 128), F32)
    weight8[:2, :] = weight_rows[...]
    weight[...] = jnp.transpose(weight8[...])

    def relay(dz):
        first_a[dz].wait_recv()
        add_rows(sa.at[dz], [part.at[me.block(1, dz), low, :], ra.at[dz]], 64)
        last_a[dz] = links.send(sa.at[dz], fl.at[dz, low, :], right)
        first_b[dz].wait_recv()
        add_rows(sb.at[dz], [part.at[me.block(3, dz), high, :], rb.at[dz]], 64)
        last_b[dz] = links.send(sb.at[dz], fr.at[dz, high, :], left)

    relay(0)
    relay(1)
    z_in[2].wait_recv()
    add_rows(s2, [part.at[me.block(2, 0), k1, :], zin.at[2]], 128)
    far_a = links.send(s2.at[low, :], ra2, right)
    far_b = links.send(s2.at[high, :], rb2, left)
    z_in[1].wait_recv()
    add_rows(s1, [part.at[me.block(1, 0), k1_high, :], zin.at[1, high, :]], 64)
    side_b = links.send(s1, fl2.at[high, :], right)
    for group in (other_b, other_a, last_a, last_b):
        group[1].wait_recv()
    add_rows(zs, [part.at[me.block(0, 1), k0, :], fl.at[1], fr.at[1]], 128)
    cross = links.send(zs, zr, pair)
    z_in[3].wait_recv()
    add_rows(s3, [part.at[me.block(3, 0), k1_low, :], zin.at[3, low, :]], 64)
    side_a = links.send(s3, fr2.at[low, :], left)
    far_a.wait_recv()
    add_rows(sa2, [part.at[me.block(1, 0), k1_low, :], zin.at[1, low, :], ra2], 64)
    end_a = links.send(sa2, fl2.at[low, :], right)
    far_b.wait_recv()
    add_rows(sb2, [part.at[me.block(3, 0), k1_high, :], zin.at[3, high, :], rb2], 64)
    end_b = links.send(sb2, fr2.at[high, :], left)

    def active(k, sources):
        @pl.loop(0, 8)
        def _(i):
            row = pl.multiple_of(i * 16, 16)
            at = pl.ds(k * 128 + row, 16)
            pre = part[me.b, at, :].astype(F32)
            for source in sources:
                pre = pre + source[pl.ds(row, 16), :].astype(F32)
            own[at, :256], own[at, 256:512], own[at, 512:] = activation(pre, weight[pl.ds(row, 16), k : k + 1])

    for group in (other_b, other_a, last_a, last_b):
        group[0].wait_recv()
    cross.wait_recv()
    active(0, [fl.at[0], fr.at[0], zr])
    mine0 = pltpu.make_async_copy(own.at[k0, :], h_out.at[me.b, k0, :], h_sem.at[0])
    mine0.start()
    from_pair = links.send(own.at[k0, :], h_out.at[me.b, k0, :], pair)
    from_left = {0: links.send(own.at[k0, :], h_out.at[me.b, k0, :], right)}
    from_right = {0: links.send(own.at[k0, :], h_out.at[me.b, k0, :], left)}

    def pass_on(block, device, rows):
        piece = h_out.at[block, rows, :]
        return links.send(piece, piece, device)

    for copy in (z_in[0], side_a, side_b, end_a, end_b):
        copy.wait_recv()
    active(1, [zin.at[0], fl2, fr2])
    mine1 = pltpu.make_async_copy(own.at[k1, :], h_out.at[me.b, k1, :], h_sem.at[1])
    mine1.start()
    left1 = links.send(own.at[k1, :], h_out.at[me.b, k1, :], right)
    right1 = links.send(own.at[k1, :], h_out.at[me.b, k1, :], left)
    tail = [links.send(own.at[k1, :], h_out.at[me.b, k1, :], pair)]
    from_pair.wait_recv()
    from_left[1] = pass_on(me.block(0, 1), right, k0)
    from_right[1] = pass_on(me.block(0, 1), left, k0)
    from_left[0].wait_recv()
    tail.append(pass_on(me.block(3, 0), right, low))
    from_right[0].wait_recv()
    tail.append(pass_on(me.block(1, 0), left, high))
    left1.wait_recv()
    half_a = pass_on(me.block(3, 0), right, k1_low)
    tail.append(pass_on(me.block(3, 0), pair, k1))
    right1.wait_recv()
    half_b = pass_on(me.block(1, 0), left, k1_high)
    tail.append(pass_on(me.block(1, 0), pair, k1))
    from_left[1].wait_recv()
    tail.append(pass_on(me.block(3, 1), right, low))
    from_right[1].wait_recv()
    tail.append(pass_on(me.block(1, 1), left, high))
    half_a.wait_recv()
    half_b.wait_recv()
    tail.append(pass_on(me.block(2, 0), pair, k1))
    for copy in tail:
        copy.wait_recv()
    mine0.wait()
    mine1.wait()


FORWARD_COPIES = 19 + 24 + 7 + 40


def forward_kernel(
    tok, og, ids_rows, weight_rows, gate_in, up_in, down_in, h_out, xt, ogt, idc, w_out,
    part, w_in, ids, x, g, ids_in, w, z_tok, z_og, l_tok, r_og, send_sem, recv_sem, own_sem, w_sem, *sums
):
    me = Spot()
    right, left, up, down = me.to(x=1), me.to(x=3), me.to(y=1), me.to(y=3)
    core, far, pair = me.to(c=1), me.to(zh=1), me.to(zl=1)
    w_in[:, :256] = gate_in[...]
    w_in[:, 256:512] = up_in[...]
    w_in[:, 512:] = jnp.transpose(down_in[...])
    ids[...] = jnp.zeros((8, 128), jnp.int32)
    ids[:2, :] = ids_rows[...]
    greet([me.to(y=dy, zl=dz) for dy, dz in PEERS] + [right, left, core, far])
    links = Links(send_sem, recv_sem)
    own, far_e = me.expert(0, 0), me.expert(0, 1)

    from_far = links.send(w_in, w.at[own, me.c], far)
    from_left0 = links.send(w_in, w.at[own, me.c], right)
    from_right0 = links.send(w_in, w.at[own, me.c], left)
    from_core = {(0, 0): [links.send(w_in, w.at[own, me.c], core)]}

    def cut(array, y, zl):
        return array.at[:, me.columns(y, zl)]

    plane = [
        links.send(cut(tok, 2, 0), l_tok.at[0], up),
        links.send(cut(og, 2, 0), r_og.at[0], down),
    ]
    z_in = {}
    z_in[2, 0] = links.send(cut(tok, 2, 1), z_tok.at[2], pair)
    z_in[2, 1] = links.send(cut(og, 2, 1), z_og.at[2], pair)
    near = []
    for y, device in ((1, up), (3, down)):
        near.append(links.send(cut(tok, y, 0), x.at[me.b], device))
        near.append(links.send(cut(og, y, 0), g.at[me.b], device))
    for y in (1, 3):
        z_in[y, 0] = links.send(cut(tok, y, 1), z_tok.at[y], pair)
        z_in[y, 1] = links.send(cut(og, y, 1), z_og.at[y], pair)
    z_in[0, 0] = links.send(cut(tok, 0, 1), x.at[me.b], pair)
    z_in[0, 1] = links.send(cut(og, 0, 1), g.at[me.b], pair)
    names = [links.send(ids, ids_in.at[me.b], me.to(y=dy, zl=dz)) for dy, dz in PEERS]
    local = [
        pltpu.make_async_copy(w_in, w.at[own, me.c], own_sem.at[0]),
        pltpu.make_async_copy(cut(tok, 0, 0), x.at[me.b], own_sem.at[1]),
        pltpu.make_async_copy(cut(og, 0, 0), g.at[me.b], own_sem.at[2]),
        pltpu.make_async_copy(ids, ids_in.at[me.b], own_sem.at[3]),
    ]
    for copy in local:
        copy.start()

    @pl.loop(0, 64)
    def _(i):
        part[i // 8, pl.ds(pl.multiple_of(i % 8 * 32, 32), 32), :] = jnp.zeros((32, 768), BF16)

    def pass_on(expert, device, rows=pl.ds(0, 384)):
        piece = w.at[expert, me.c, rows, :]
        return links.send(piece, piece, device)

    low, high = pl.ds(0, 192), pl.ds(192, 192)
    across, ends = [], []
    z_in[2, 0].wait_recv()
    across.append(links.send(z_tok.at[2], l_tok.at[1], up))
    plane[0].wait_recv()
    ends.append(links.send(l_tok.at[0], x.at[me.block(3, 0)], up))
    z_in[2, 1].wait_recv()
    across.append(links.send(z_og.at[2], r_og.at[1], down))
    plane[1].wait_recv()
    ends.append(links.send(r_og.at[0], g.at[me.block(1, 0)], down))
    halves = {0: [], 1: []}

    def sideways(dz, from_left, from_right):
        from_left.wait_recv()
        halves[dz].append(pass_on(me.expert(3, dz), right, low))
        from_core[3, dz] = [pass_on(me.expert(3, dz), core)]
        from_right.wait_recv()
        halves[dz].append(pass_on(me.expert(1, dz), left, high))
        from_core[1, dz] = [pass_on(me.expert(1, dz), core)]

    sideways(0, from_left0, from_right0)
    late = []

    def partner(y, device):
        z_in[y, 0].wait_recv()
        late.append(links.send(z_tok.at[y], x.at[me.block(0, 1)], device))
        z_in[y, 1].wait_recv()
        late.append(links.send(z_og.at[y], g.at[me.block(0, 1)], device))

    partner(1, up)
    from_far.wait_recv()
    from_left1 = pass_on(far_e, right)
    from_right1 = pass_on(far_e, left)
    from_core[0, 1] = [pass_on(far_e, core)]
    partner(3, down)
    across[0].wait_recv()
    late.append(links.send(l_tok.at[1], x.at[me.block(3, 1)], up))
    across[1].wait_recv()
    late.append(links.send(r_og.at[1], g.at[me.block(1, 1)], down))

    def second(dz):
        from_core[2, dz] = []
        for n, half in enumerate(halves[dz]):
            half.wait_recv()
            from_core[2, dz].append(pass_on(me.expert(2, dz), core, (low, high)[n]))

    def turn(dz):
        for y in range(4):
            b = me.block(y, dz)
            at = pl.ds(pl.multiple_of(b * 128, 128), 128)
            xt[:, at] = jnp.transpose(x[b])
            ogt[:, at] = jnp.transpose(g[b])
            idc[at, :] = jnp.transpose(ids_in[b])

    def keep(step, dz):
        for copy in from_core[step, dz]:
            copy.wait_recv()
        e = me.expert(step, dz)
        pltpu.make_async_copy(w.at[e], w_out.at[e], w_sem.at[e]).start()

    def product(e, dz):
        plane_at = pl.multiple_of((me.zl + dz) % 2 * 4, 4)
        for n, source in ((0, x), (1, x), (2, g)):
            cols = slice(n * 256, n * 256 + 256)
            rows = source[pl.ds(plane_at, 4)].reshape(512, 768)
            out = jnp.dot(rows, w[e, :, :, cols].reshape(768, 256), preferred_element_type=F32)
            for y in range(4):
                names_at = pl.ds(pl.multiple_of((plane_at + y) * 128, 128), 128)
                for k in range(2):
                    here = part.at[plane_at + y, k * 128 : k * 128 + 128, cols]
                    chosen = idc[names_at, k : k + 1] == e
                    old = here[...].astype(F32)
                    here[...] = jnp.where(chosen, out[y * 128 : y * 128 + 128], old).astype(BF16)

    def first_six(i):
        g2 = i // 2
        step = (g2 + 1) // 2 * (1 + 2 * (i % 2))
        return me.expert(step, (1 - (g2 + 1) // 2) * (i % 2) + g2 // 2)

    for copy in near + ends + names:
        copy.wait_recv()
    for copy in local:
        copy.wait()
    turn(0)
    for step, dz in ((0, 0), (0, 1), (1, 0), (3, 0)):
        keep(step, dz)

    @pl.loop(0, 4)
    def _(i):
        product(first_six(i), 0)

    second(0)
    sideways(1, from_left1, from_right1)
    keep(1, 1)
    keep(3, 1)

    @pl.loop(4, 6)
    def _(i):
        product(first_six(i), 0)

    second(1)
    keep(2, 0)
    keep(2, 1)

    @pl.loop(0, 2)
    def _(i):
        product(me.expert(2, i), 0)

    opened = {0: open_sums(me, links, part, 0, sums)}
    for copy in [z_in[0, 0], z_in[0, 1]] + late:
        copy.wait_recv()
    turn(1)

    @pl.loop(0, 8)
    def _(i):
        product(i, 1)

    close_sums(me, links, part, weight_rows, h_out, opened, sums)
    links.finish()
    for e in range(8):
        pltpu.make_async_copy(w.at[e], w_out.at[e], w_sem.at[e]).wait()


def forward(tokens, out_grad, ids, weight, w_gate, w_up, w_down):
    vmem, anywhere = pl.BlockSpec(memory_space=pltpu.VMEM), pl.BlockSpec(memory_space=pl.ANY)
    blocks = lambda n: pltpu.VMEM((n, 128, 768), BF16)
    rows = lambda *shape: pltpu.VMEM(shape + (768,), BF16)
    return pl.pallas_call(
        forward_kernel,
        out_shape=(
            jax.ShapeDtypeStruct((8, 256, 768), BF16),
            jax.ShapeDtypeStruct((768, 1024), BF16),
            jax.ShapeDtypeStruct((768, 1024), BF16),
            jax.ShapeDtypeStruct((1024, 8), jnp.int32),
            jax.ShapeDtypeStruct((8, 2, 384, 768), BF16),
        ),
        in_specs=[vmem] * 7,
        out_specs=(anywhere,) + (vmem,) * 3 + (anywhere,),
        scratch_shapes=[
            pltpu.VMEM((8, 256, 768), BF16),
            pltpu.VMEM((384, 768), BF16),
            pltpu.VMEM((8, 128), jnp.int32),
            blocks(8),
            blocks(8),
            pltpu.VMEM((8, 8, 128), jnp.int32),
            pltpu.VMEM((8, 2, 384, 768), BF16),
            blocks(4),
            blocks(4),
            blocks(2),
            blocks(2),
            pltpu.SemaphoreType.DMA((FORWARD_COPIES,)),
            pltpu.SemaphoreType.DMA((FORWARD_COPIES,)),
            pltpu.SemaphoreType.DMA((4,)),
            pltpu.SemaphoreType.DMA((8,)),
            pltpu.VMEM((8, 128), F32),
            pltpu.VMEM((128, 8), F32),
        ]
        + [rows(2, 64)] * 4
        + [rows(2, 128)] * 2
        + [rows(128)] * 2
        + [rows(4, 128), rows(128)]
        + [rows(64)] * 6
        + [rows(128)] * 2
        + [rows(256), pltpu.SemaphoreType.DMA((2,))],
        compiler_params=pltpu.CompilerParams(collective_id=0, has_side_effects=True, vmem_limit_bytes=60 << 20),
        name="forward",
    )(tokens, out_grad, ids, weight, w_gate, w_up, w_down)


FINISH_COPIES = 8 + 4 + 4 + 4 + 1 + 16


def finish_kernel(
    xt, ogt, ids, h, w, d_out, gate_out, up_out, down_out,
    w_all, he, g, cr, dx, g_out, zd, dl, dr, a2, ra, rb, sa, sb, oa, ob, fl, fr, zs, zr,
    send_sem, recv_sem, w_sem, own_sem,
):
    me = Spot()
    right, left, core, far = me.to(x=1), me.to(x=3), me.to(c=1), me.to(zh=1)
    up, down, pair = me.to(y=1), me.to(y=3), me.to(zl=1)
    loads = [pltpu.make_async_copy(w.at[e], w_all.at[e], w_sem.at[e]) for e in range(8)]
    for load in loads:
        load.start()
    greet([up, down, pair, right, left, core, far])
    links = Links(send_sem, recv_sem)
    low, high = pl.ds(0, 192), pl.ds(192, 192)
    mine, others = me.c, 1 - me.c
    swapped, first_a, first_b, other_b, other_a, last_a, last_b = {}, {}, {}, {}, {}, {}, {}

    def fill(step, dz):
        e = me.expert(step, dz)

        @pl.loop(0, 8)
        def _(q):
            at = pl.ds(pl.multiple_of(q * 128, 128), 128)
            chosen = [(ids[at, k : k + 1] == e).astype(F32) for k in range(2)]
            m0, m1 = [jnp.broadcast_to(m, (128, 128)).astype(BF16) for m in chosen]
            for n in range(6):
                cols = slice(n * 128, n * 128 + 128)
                he[e, at, cols] = h[q, :128, cols] * m0 + h[q, 128:, cols] * m1

    def product(step, dz):
        e = me.expert(step, dz)
        for n, left_t in ((0, xt), (1, xt), (2, ogt)):
            cols = slice(n * 256, n * 256 + 256)
            out = jnp.dot(left_t[...], he[e, :, cols], preferred_element_type=F32).astype(BF16)
            g[e, 0, :, cols] = out[:384]
            g[e, 1, :, cols] = out[384:]
        swapped[step, dz] = links.send(g.at[e, others], cr.at[e], core)

    def start_far(dz):
        e = me.expert(2, dz)
        swapped[2, dz].wait_recv()
        add_rows(a2.at[dz], [g.at[e, mine], cr.at[e]], 384)
        first_a[dz] = links.send(a2.at[dz, low, :], ra.at[dz], right)
        first_b[dz] = links.send(a2.at[dz, high, :], rb.at[dz], left)

    def start_near(dz):
        e = me.expert(1, dz)
        swapped[1, dz].wait_recv()
        add_rows(ob.at[dz], [g.at[e, mine, high, :], cr.at[e, high, :]], 192)
        other_b[dz] = links.send(ob.at[dz], fl.at[dz, high, :], right)
        e = me.expert(3, dz)
        swapped[3, dz].wait_recv()
        add_rows(oa.at[dz], [g.at[e, mine, low, :], cr.at[e, low, :]], 192)
        other_a[dz] = links.send(oa.at[dz], fr.at[dz, low, :], left)

    def relay(dz):
        e = me.expert(1, dz)
        first_a[dz].wait_recv()
        add_rows(sa.at[dz], [g.at[e, mine, low, :], cr.at[e, low, :], ra.at[dz]], 192)
        last_a[dz] = links.send(sa.at[dz], fl.at[dz, low, :], right)
        e = me.expert(3, dz)
        first_b[dz].wait_recv()
        add_rows(sb.at[dz], [g.at[e, mine, high, :], cr.at[e, high, :], rb.at[dz]], 192)
        last_b[dz] = links.send(sb.at[dz], fr.at[dz, high, :], left)

    def token_part(n):
        cols = slice(n * 256, n * 256 + 256)
        total = None
        for e in range(8):
            part = lax.dot_general(
                he[e, :, :512], w_all[e, cols, :512], (((1,), (1,)), ((), ())), preferred_element_type=F32
            )
            total = part if total is None else total + part
        for q in range(8):
            dx[q, :, cols] = total[q * 128 : q * 128 + 128].astype(BF16)

    for step in (2, 1):
        fill(step, 1)
        product(step, 1)
    start_far(1)
    fill(3, 1)
    product(3, 1)
    for step, dz in ((0, 1), (0, 0), (1, 0)):
        fill(step, dz)
    start_near(1)
    for step in (2, 3):
        fill(step, 0)
    for load in loads:
        load.wait()
    token_part(0)
    token_part(1)
    relay(1)
    token_part(2)

    first, last = pl.ds(0, 64), pl.ds(64, 64)
    columns = lambda y, zl: d_out.at[:, me.columns(y, zl)]
    l_in = {0: links.send(dx.at[me.block(2, 0), first, :], dl.at[0], up)}
    r_in = {0: links.send(dx.at[me.block(2, 0), last, :], dr.at[0], down)}
    z_in = {y: links.send(dx.at[me.block(y, 1)], zd.at[y], pair) for y in (2, 1, 3)}
    back = [
        links.send(dx.at[me.block(0, 1)], columns(0, 0), pair),
        links.send(dx.at[me.block(1, 0)], columns(0, 0), up),
        links.send(dx.at[me.block(3, 0)], columns(0, 0), down),
    ]
    keep = pltpu.make_async_copy(dx.at[me.b], columns(0, 0), own_sem)
    keep.start()

    def hand_on(dz):
        l_in[dz].wait_recv()
        back.append(links.send(dl.at[dz], d_out.at[first, me.columns(3, dz)], up))
        r_in[dz].wait_recv()
        back.append(links.send(dr.at[dz], d_out.at[last, me.columns(1, dz)], down))

    product(2, 0)
    product(1, 0)
    start_far(0)
    product(3, 0)
    z_in[2].wait_recv()
    l_in[1] = links.send(zd.at[2, first, :], dl.at[1], up)
    r_in[1] = links.send(zd.at[2, last, :], dr.at[1], down)
    hand_on(0)
    start_near(0)
    product(0, 1)
    z_in[1].wait_recv()
    back.append(links.send(zd.at[1], columns(0, 1), up))
    for group in (other_b, other_a, last_a, last_b):
        group[1].wait_recv()
    e = me.expert(0, 1)
    swapped[0, 1].wait_recv()
    add_rows(zs, [g.at[e, mine], cr.at[e], fl.at[1], fr.at[1]], 384)
    cross = links.send(zs, zr, far)
    z_in[3].wait_recv()
    back.append(links.send(zd.at[3], columns(0, 1), down))
    product(0, 0)
    hand_on(1)
    relay(0)
    for group in (other_b, other_a, last_a, last_b):
        group[0].wait_recv()
    swapped[0, 0].wait_recv()
    cross.wait_recv()
    e = me.expert(0, 0)
    add_rows(g_out, [g.at[e, mine], cr.at[e], fl.at[0], fr.at[0], zr], 384)
    gate_out[...] = g_out[:, :256]
    up_out[...] = g_out[:, 256:512]
    down_out[...] = jnp.transpose(g_out[:, 512:])
    for copy in back:
        copy.wait_recv()
    keep.wait()
    links.finish()


def finish(xt, ogt, ids, h, w):
    vmem, anywhere = pl.BlockSpec(memory_space=pltpu.VMEM), pl.BlockSpec(memory_space=pl.ANY)
    half, full = pltpu.VMEM((2, 192, 768), BF16), pltpu.VMEM((2, 384, 768), BF16)
    one = pltpu.VMEM((384, 768), BF16)
    return pl.pallas_call(
        finish_kernel,
        out_shape=(
            jax.ShapeDtypeStruct((128, 6144), BF16),
            jax.ShapeDtypeStruct((384, 256), F32),
            jax.ShapeDtypeStruct((384, 256), F32),
            jax.ShapeDtypeStruct((256, 384), F32),
        ),
        in_specs=[vmem] * 4 + [anywhere],
        out_specs=(anywhere,) + (vmem,) * 3,
        scratch_shapes=[
            pltpu.VMEM((8, 768, 768), BF16),
            pltpu.VMEM((8, 1024, 768), BF16),
            pltpu.VMEM((8, 2, 384, 768), BF16),
            pltpu.VMEM((8, 384, 768), BF16),
            pltpu.VMEM((8, 128, 768), BF16),
            pltpu.VMEM((384, 768), F32),
            pltpu.VMEM((4, 128, 768), BF16),
            pltpu.VMEM((2, 64, 768), BF16),
            pltpu.VMEM((2, 64, 768), BF16),
        ]
        + [full] + [half] * 6 + [full] * 2 + [one] * 2
        + [
            pltpu.SemaphoreType.DMA((FINISH_COPIES,)),
            pltpu.SemaphoreType.DMA((FINISH_COPIES,)),
            pltpu.SemaphoreType.DMA((8,)),
            pltpu.SemaphoreType.DMA,
        ],
        compiler_params=pltpu.CompilerParams(collective_id=2, has_side_effects=True, vmem_limit_bytes=60 << 20),
        name="finish",
    )(xt, ogt, ids, h, w)


def shards(tokens, out_grad, expert_ids, route_weight, w_gate, w_up, w_down):
    ids, weight = jnp.transpose(expert_ids), jnp.transpose(route_weight)
    h, xt, ogt, names, w = forward(tokens, out_grad, ids, weight, w_gate[0], w_up[0], w_down[0])
    d_tokens, gate, up, down = finish(xt, ogt, names, h, w.reshape(8, 768, 768))
    return d_tokens, gate[None], up[None], down[None]


def solution(mesh):
    in_specs = (
        P(("dp", "ep"), None),
        P(("dp", "ep"), None),
        P(("dp", "ep"), None),
        P(("dp", "ep"), None),
        P("ep", "dp", None),
        P("ep", "dp", None),
        P("ep", None, "dp"),
    )
    out_specs = (
        P(("dp", "ep"), None),
        P("ep", "dp", None),
        P("ep", "dp", None),
        P("ep", None, "dp"),
    )
    return jax.shard_map(shards, mesh=mesh, in_specs=in_specs, out_specs=out_specs, check_vma=False)
```

time: 208 us -> 202 us (0.971)
  Pallas kernels: 202 us -> 196 us
    pallas_call x1, Pallas kernels: 72.6 us -> 62.4 us  [finish(): pl.pallas_call(finish_kernel, out_shape=(jax.ShapeDtypeStruct((128, 6144)...]
    pallas_call x2 -> x1, Pallas kernels: 130 us -> 133 us  [forward(): pl.pallas_call(forward_kernel, out_shape=(jax.ShapeDtypeStruct((8, 256, 7...]
where the time goes in v3:
time: 202 us
  Pallas kernels  196 us (97%)
  local copies, waits for them, and re-layouts  5.03 us (2%)
    pallas_call x1, Pallas kernels, forward(): pl.pallas_call(forward_kernel, out_shape=(jax.ShapeDtypeStruct((8, 256, 7...  133 us
    pallas_call x1, Pallas kernels, finish(): pl.pallas_call(finish_kernel, out_shape=(jax.ShapeDtypeStruct((128, 6144)...  62.4 us
    unnamed x10, local copies, waits for them, and re-layouts  5.03 us

profile of v3, /device:TPU:1, one launch (start us, length us, event | category | flops | bytes accessed | tf_op | source)
XLA Modules:
  0.0 201.6 jit_solution(2241154285641509294)
XLA Ops:
  0.6 133.5 %forward.1 = (bf16[8,256,768]{2,1,0:T(8,128)(2,1)}, bf16[768,1024]{1,0:T(8,128)(2,1)}, bf16[768,1024]{1,0:T(8,128)(2,1)}, s32[1024,8]{1,0:T(8,128)}, bf16[8,2,384,768]{3,2,1,0:T(8,128)(2,1)}) custom-call(bf16[128,6144]{1,0:T(8,128)(2,1)} %tok.1, bf16[128,6144]{1,0:T(8,128)(2,1)} %og.1, s32[2,128]{1,0:T(2,128)} %bitcast.16, f32[2,128]{1,0:T(2,128)} %bitcast.17, ...), custom_call_target="tpu_custom_call" | custom-call | tf_op jit(solution)/shard_map/forward/pallas_call | solution.py:395
  134.1 62.4 %finish.1 = (bf16[128,6144]{1,0:T(8,128)(2,1)}, f32[384,256]{1,0:T(8,128)}, f32[384,256]{1,0:T(8,128)}, f32[256,384]{1,0:T(8,128)}) custom-call(bf16[768,1024]{1,0:T(8,128)(2,1)} %get-tuple-element.13.xt, bf16[768,1024]{1,0:T(8,128)(2,1)} %get-tuple-element.14.ogt, s32[1024,8]{1,0:T(8,128)} %get-tuple-element.15.ids, ...), custom_call_target="tpu_custom_call" | custom-call | tf_op jit(solution)/shard_map/finish/pallas_call | solution.py:595
  196.5 0.0 copy-start.2
  196.5 0.0 copy-start.1
  196.5 0.0 copy-start
  196.5 2.8 %copy.15 = bf16[128,6144]{1,0:T(8,128)(2,1)} copy(bf16[128,6144]{1,0:T(8,128)(2,1)} %get-tuple-element.26) | data formatting | bytes 3145728
  199.3 0.0 copy-done.2
  199.3 0.7 copy.16
  200.1 0.0 copy-done.1
  200.1 0.7 copy.17
  200.8 0.0 copy-done
  200.8 0.7 copy.18
Async XLA Ops:
  196.5 2.8 %copy-start.2 = (f32[384,256]{1,0:T(8,128)S(1)}, f32[384,256]{1,0:T(8,128)}, u32[]{:S(2)}) copy-start(f32[384,256]{1,0:T(8,128)} %get-tuple-element.19) | copy-start | bytes 1179652
  196.5 3.6 %copy-start.1 = (f32[384,256]{1,0:T(8,128)S(1)}, f32[384,256]{1,0:T(8,128)}, u32[]{:S(2)}) copy-start(f32[384,256]{1,0:T(8,128)} %get-tuple-element.20) | copy-start | bytes 1179652
  196.5 4.3 %copy-start = (f32[256,384]{1,0:T(8,128)S(1)}, f32[256,384]{1,0:T(8,128)}, u32[]{:S(2)}) copy-start(f32[256,384]{1,0:T(8,128)} %get-tuple-element.21) | copy-start | bytes 1179652

commit v4 on v3

--- a/solution.py
+++ b/solution.py
@@ -98,7 +98,7 @@
     )
 
 
-def close_sums(me, links, part, weight_rows, h_out, opened, sums):
+def close_sums(me, links, part, weight_rows, h_out, opened, sums, meanwhile):
     (
         weight8, weight, ra, rb, sa, sb, fl, fr, zs, zr, zin, s2, s1, s3, ra2, rb2, sa2, sb2, fl2, fr2, own, h_sem,
     ) = sums
@@ -114,6 +114,7 @@
     weight8[...] = jnp.zeros((8, 128), F32)
     weight8[:2, :] = weight_rows[...]
     weight[...] = jnp.transpose(weight8[...])
+    meanwhile()
 
     def relay(dz):
         first_a[dz].wait_recv()
@@ -294,11 +295,11 @@
         z_in[y, 1].wait_recv()
         late.append(links.send(z_og.at[y], g.at[me.block(0, 1)], device))
 
-    partner(1, up)
     from_far.wait_recv()
     from_left1 = pass_on(far_e, right)
     from_right1 = pass_on(far_e, left)
     from_core[0, 1] = [pass_on(far_e, core)]
+    partner(1, up)
     partner(3, down)
     across[0].wait_recv()
     late.append(links.send(l_tok.at[1], x.at[me.block(3, 1)], up))
@@ -317,6 +318,11 @@
             at = pl.ds(pl.multiple_of(b * 128, 128), 128)
             xt[:, at] = jnp.transpose(x[b])
             ogt[:, at] = jnp.transpose(g[b])
+
+    def name_rows(dz):
+        for y in range(4):
+            b = me.block(y, dz)
+            at = pl.ds(pl.multiple_of(b * 128, 128), 128)
             idc[at, :] = jnp.transpose(ids_in[b])
 
     def keep(step, dz):
@@ -349,6 +355,7 @@
     for copy in local:
         copy.wait()
     turn(0)
+    name_rows(0)
     for step, dz in ((0, 0), (0, 1), (1, 0), (3, 0)):
         keep(step, dz)
 
@@ -365,6 +372,14 @@
     def _(i):
         product(first_six(i), 0)
 
+    for copy in [z_in[0, 0], z_in[0, 1]] + late:
+        copy.wait_recv()
+    name_rows(1)
+
+    @pl.loop(0, 6)
+    def _(i):
+        product(first_six(i), 1)
+
     second(1)
     keep(2, 0)
     keep(2, 1)
@@ -374,15 +389,12 @@
         product(me.expert(2, i), 0)
 
     opened = {0: open_sums(me, links, part, 0, sums)}
-    for copy in [z_in[0, 0], z_in[0, 1]] + late:
-        copy.wait_recv()
-    turn(1)
-
-    @pl.loop(0, 8)
+
+    @pl.loop(0, 2)
     def _(i):
-        product(i, 1)
-
-    close_sums(me, links, part, weight_rows, h_out, opened, sums)
+        product(me.expert(2, i), 1)
+
+    close_sums(me, links, part, weight_rows, h_out, opened, sums, lambda: turn(1))
     links.finish()
     for e in range(8):
         pltpu.make_async_copy(w.at[e], w_out.at[e], w_sem.at[e]).wait()
@@ -438,15 +450,17 @@
 
 
 def finish_kernel(
-    xt, ogt, ids, h, w, d_out, gate_out, up_out, down_out,
-    w_all, he, g, cr, dx, g_out, zd, dl, dr, a2, ra, rb, sa, sb, oa, ob, fl, fr, zs, zr,
+    xt_in, ogt_in, ids_in, h_in, w, d_out, gate_out, up_out, down_out,
+    xt, ogt, ids, h, w_all, he, g, cr, dx, g_out, zd, dl, dr, a2, ra, rb, sa, sb, oa, ob, fl, fr, zs, zr,
     send_sem, recv_sem, w_sem, own_sem,
 ):
     me = Spot()
     right, left, core, far = me.to(x=1), me.to(x=3), me.to(c=1), me.to(zh=1)
     up, down, pair = me.to(y=1), me.to(y=3), me.to(zl=1)
+    sources = ((ids_in, ids), (h_in, h), (xt_in, xt), (ogt_in, ogt))
+    heads = [pltpu.make_async_copy(src, dst, w_sem.at[8 + n]) for n, (src, dst) in enumerate(sources)]
     loads = [pltpu.make_async_copy(w.at[e], w_all.at[e], w_sem.at[e]) for e in range(8)]
-    for load in loads:
+    for load in heads + loads:
         load.start()
     greet([up, down, pair, right, left, core, far])
     links = Links(send_sem, recv_sem)
@@ -513,6 +527,8 @@
         for q in range(8):
             dx[q, :, cols] = total[q * 128 : q * 128 + 128].astype(BF16)
 
+    for load in heads:
+        load.wait()
     for step in (2, 1):
         fill(step, 1)
         product(step, 1)
@@ -600,9 +616,13 @@
             jax.ShapeDtypeStruct((384, 256), F32),
             jax.ShapeDtypeStruct((256, 384), F32),
         ),
-        in_specs=[vmem] * 4 + [anywhere],
+        in_specs=[anywhere] * 5,
         out_specs=(anywhere,) + (vmem,) * 3,
         scratch_shapes=[
+            pltpu.VMEM((768, 1024), BF16),
+            pltpu.VMEM((768, 1024), BF16),
+            pltpu.VMEM((1024, 8), jnp.int32),
+            pltpu.VMEM((8, 256, 768), BF16),
             pltpu.VMEM((8, 768, 768), BF16),
             pltpu.VMEM((8, 1024, 768), BF16),
             pltpu.VMEM((8, 2, 384, 768), BF16),
@@ -617,7 +637,7 @@
         + [
             pltpu.SemaphoreType.DMA((FINISH_COPIES,)),
             pltpu.SemaphoreType.DMA((FINISH_COPIES,)),
-            pltpu.SemaphoreType.DMA((8,)),
+            pltpu.SemaphoreType.DMA((12,)),
             pltpu.SemaphoreType.DMA,
         ],
         compiler_params=pltpu.CompilerParams(collective_id=2, has_side_effects=True, vmem_limit_bytes=60 << 20),
@@ -625,10 +645,43 @@
     )(xt, ogt, ids, h, w)
 
 
+def deliver_kernel(*refs):
+    sources, results, places = refs[:4], refs[4:8], refs[8:12]
+    in_sem, out_sem = refs[12:]
+    pieces = []
+    for n in range(4):
+        rows = sources[n].shape[0]
+        step = 32 if n == 0 else rows
+        for row in range(0, rows, step):
+            pieces.append((n, pl.ds(row, step)))
+    fetch = [pltpu.make_async_copy(sources[n].at[at], places[n].at[at], in_sem.at[i]) for i, (n, at) in enumerate(pieces)]
+    store = [pltpu.make_async_copy(places[n].at[at], results[n].at[at], out_sem.at[i]) for i, (n, at) in enumerate(pieces)]
+    for copy in fetch:
+        copy.start()
+    for first, second in zip(fetch, store):
+        first.wait()
+        second.start()
+    for copy in store:
+        copy.wait()
+
+
+def deliver(*arrays):
+    anywhere = pl.BlockSpec(memory_space=pl.ANY)
+    return pl.pallas_call(
+        deliver_kernel,
+        out_shape=tuple(jax.ShapeDtypeStruct(a.shape, a.dtype) for a in arrays),
+        in_specs=[anywhere] * 4,
+        out_specs=(anywhere,) * 4,
+        scratch_shapes=[pltpu.VMEM(a.shape, a.dtype) for a in arrays]
+        + [pltpu.SemaphoreType.DMA((7,)), pltpu.SemaphoreType.DMA((7,))],
+        name="deliver",
+    )(*arrays)
+
+
 def shards(tokens, out_grad, expert_ids, route_weight, w_gate, w_up, w_down):
     ids, weight = jnp.transpose(expert_ids), jnp.transpose(route_weight)
     h, xt, ogt, names, w = forward(tokens, out_grad, ids, weight, w_gate[0], w_up[0], w_down[0])
-    d_tokens, gate, up, down = finish(xt, ogt, names, h, w.reshape(8, 768, 768))
+    d_tokens, gate, up, down = deliver(*finish(xt, ogt, names, h, w.reshape(8, 768, 768)))
     return d_tokens, gate[None], up[None], down[None]
 
 

time: 202 us -> 194 us (0.960)
  local copies, waits for them, and re-layouts: 5.03 us -> 0 us
  Pallas kernels: 196 us -> 192 us
    pallas_call x1, Pallas kernels: 133 us -> 125 us  [forward(): pl.pallas_call(forward_kernel, out_shape=(jax.ShapeDtypeStruct((8, 256, 7...]
    unnamed x10 -> x0, local copies, waits for them, and re-layouts: 5.03 us -> none
    pallas_call x0 -> x1, Pallas kernels: none -> 2.64 us  [deliver(): pl.pallas_call(deliver_kernel, out_shape=tuple((jax.ShapeDtypeStruct(a.sh...]
    pallas_call x1, Pallas kernels: 62.4 us -> 64.4 us  [finish(): pl.pallas_call(finish_kernel, out_shape=(jax.ShapeDtypeStruct((128, 6144)...]
where the time goes in v4:
time: 194 us; the launch traced here: 193 us
  Pallas kernels  192 us (99%)
    pallas_call x1, Pallas kernels, forward(): pl.pallas_call(forward_kernel, out_shape=(jax.ShapeDtypeStruct((8, 256, 7...  125 us
    pallas_call x1, Pallas kernels, finish(): pl.pallas_call(finish_kernel, out_shape=(jax.ShapeDtypeStruct((128, 6144)...  64.4 us

profile of v4, /device:TPU:1, one launch (start us, length us, event | category | flops | bytes accessed | tf_op | source)
XLA Modules:
  0.0 192.9 jit_solution(155119776632710883)
XLA Ops:
  0.6 125.0 %forward.1 = (bf16[8,256,768]{2,1,0:T(8,128)(2,1)}, bf16[768,1024]{1,0:T(8,128)(2,1)}, bf16[768,1024]{1,0:T(8,128)(2,1)}, s32[1024,8]{1,0:T(8,128)}, bf16[8,2,384,768]{3,2,1,0:T(8,128)(2,1)}) custom-call(bf16[128,6144]{1,0:T(8,128)(2,1)} %tok.1, bf16[128,6144]{1,0:T(8,128)(2,1)} %og.1, s32[2,128]{1,0:T(2,128)} %bitcast.13, f32[2,128]{1,0:T(2,128)} %bitcast.14, ...), custom_call_target="tpu_custom_call" | custom-call | tf_op jit(solution)/shard_map/forward/pallas_call | solution.py:407
  125.7 64.4 %finish.1 = (bf16[128,6144]{1,0:T(8,128)(2,1)}, f32[384,256]{1,0:T(8,128)}, f32[384,256]{1,0:T(8,128)}, f32[256,384]{1,0:T(8,128)}) custom-call(bf16[768,1024]{1,0:T(8,128)(2,1)} %get-tuple-element.17.xt_in, bf16[768,1024]{1,0:T(8,128)(2,1)} %get-tuple-element.18.ogt_in, s32[1024,8]{1,0:T(8,128)} %get-tuple-element.19.ids_in, ...), custom_call_target="tpu_custom_call" | custom-call | tf_op jit(solution)/shard_map/finish/pallas_call | solution.py:611
  190.1 2.6 %deliver.1 = (bf16[128,6144]{1,0:T(8,128)(2,1)}, f32[384,256]{1,0:T(8,128)}, f32[384,256]{1,0:T(8,128)}, f32[256,384]{1,0:T(8,128)}) custom-call(bf16[128,6144]{1,0:T(8,128)(2,1)} %get-tuple-element.22.refs_0_, f32[384,256]{1,0:T(8,128)} %get-tuple-element.23.refs_1_, f32[384,256]{1,0:T(8,128)} %get-tuple-element.24.refs_2_, ...), custom_call_target="tpu_custom_call" | custom-call | tf_op jit(solution)/shard_map/deliver/pallas_call | solution.py:670

commit v5 on v4

--- a/solution.py
+++ b/solution.py
@@ -114,7 +114,6 @@
     weight8[...] = jnp.zeros((8, 128), F32)
     weight8[:2, :] = weight_rows[...]
     weight[...] = jnp.transpose(weight8[...])
-    meanwhile()
 
     def relay(dz):
         first_a[dz].wait_recv()
@@ -125,6 +124,7 @@
         last_b[dz] = links.send(sb.at[dz], fr.at[dz, high, :], left)
 
     relay(0)
+    meanwhile()
     relay(1)
     z_in[2].wait_recv()
     add_rows(s2, [part.at[me.block(2, 0), k1, :], zin.at[2]], 128)
@@ -586,9 +586,9 @@
     cross = links.send(zs, zr, far)
     z_in[3].wait_recv()
     back.append(links.send(zd.at[3], columns(0, 1), down))
+    relay(0)
     product(0, 0)
     hand_on(1)
-    relay(0)
     for group in (other_b, other_a, last_a, last_b):
         group[0].wait_recv()
     swapped[0, 0].wait_recv()

time: 194 us -> 194 us (level)
  no operation moved by 1% of the time
where the time goes in v5:
time: 194 us; the launch traced here: 193 us
  Pallas kernels  192 us (99%)
    pallas_call x1, Pallas kernels, forward(): pl.pallas_call(forward_kernel, out_shape=(jax.ShapeDtypeStruct((8, 256, 7...  125 us
    pallas_call x1, Pallas kernels, finish(): pl.pallas_call(finish_kernel, out_shape=(jax.ShapeDtypeStruct((128, 6144)...  64.4 us

profile of v5, /device:TPU:1, one launch (start us, length us, event | category | flops | bytes accessed | tf_op | source)
XLA Modules:
  0.0 192.9 jit_solution(14877527460803230468)
XLA Ops:
  0.6 125.0 %forward.1 = (bf16[8,256,768]{2,1,0:T(8,128)(2,1)}, bf16[768,1024]{1,0:T(8,128)(2,1)}, bf16[768,1024]{1,0:T(8,128)(2,1)}, s32[1024,8]{1,0:T(8,128)}, bf16[8,2,384,768]{3,2,1,0:T(8,128)(2,1)}) custom-call(bf16[128,6144]{1,0:T(8,128)(2,1)} %tok.1, bf16[128,6144]{1,0:T(8,128)(2,1)} %og.1, s32[2,128]{1,0:T(2,128)} %bitcast.13, f32[2,128]{1,0:T(2,128)} %bitcast.14, ...), custom_call_target="tpu_custom_call" | custom-call | tf_op jit(solution)/shard_map/forward/pallas_call | solution.py:407
  125.7 64.4 %finish.1 = (bf16[128,6144]{1,0:T(8,128)(2,1)}, f32[384,256]{1,0:T(8,128)}, f32[384,256]{1,0:T(8,128)}, f32[256,384]{1,0:T(8,128)}) custom-call(bf16[768,1024]{1,0:T(8,128)(2,1)} %get-tuple-element.17.xt_in, bf16[768,1024]{1,0:T(8,128)(2,1)} %get-tuple-element.18.ogt_in, s32[1024,8]{1,0:T(8,128)} %get-tuple-element.19.ids_in, ...), custom_call_target="tpu_custom_call" | custom-call | tf_op jit(solution)/shard_map/finish/pallas_call | solution.py:611
  190.1 2.6 %deliver.1 = (bf16[128,6144]{1,0:T(8,128)(2,1)}, f32[384,256]{1,0:T(8,128)}, f32[384,256]{1,0:T(8,128)}, f32[256,384]{1,0:T(8,128)}) custom-call(bf16[128,6144]{1,0:T(8,128)(2,1)} %get-tuple-element.22.refs_0_, f32[384,256]{1,0:T(8,128)} %get-tuple-element.23.refs_1_, f32[384,256]{1,0:T(8,128)} %get-tuple-element.24.refs_2_, ...), custom_call_target="tpu_custom_call" | custom-call | tf_op jit(solution)/shard_map/deliver/pallas_call | solution.py:670
